TPU v7x, 32 devices: a whole 2x2x4 slice. The times are simulated.
32 devices in a mesh: gx: 2 (over y), gy: 4 (over z), gz: 4 (over x, core).
Axes of the slice: x: 2, y: 2, z: 4, core: 2. Of those that a mesh axis runs over, the one named last changes fastest.
Arguments:
- right_side: float32 [32, 64, 512], P('gx', 'gy', 'gz'), may hold values from -6 to 6
- coefficient: float32 [32, 64, 512], P('gx', 'gy', 'gz'), may hold values from 0.5 to 4
- start_vector: float32 [32, 64, 512], P('gx', 'gy', 'gz'), may hold values from -12 to 12
- plane_counts: int32 [4], replicated, may hold values from 32 to 128, as said below
Outputs:
- solution_field: float32 [32, 64, 512], P('gx', 'gy', 'gz')
- residual: float32 [32, 64, 512], P('gx', 'gy', 'gz')
Inputs may be any that keep to these rules, and one draw needn't show every extreme that they name: plane_counts sum to 320, and the largest is exactly 128.
All inputs are finite; a program needn't handle non-finite values.
Results may differ from a plain program's by a relative error of at most 0.0003.
Values sent between devices are 32-bit elements; how exact they have to be, the bound alone decides.
A program may use at most 64 MiB of HBM per device.

v0:
```python
import jax
import jax.numpy as jnp
from jax import lax
from jax.sharding import PartitionSpec as P

POWER = 3
DEGREE = 4


def padded(cells, sides, width):
    for axis, dim in sides:
        count = lax.axis_size(axis)
        ends = count - 1
        head = lax.slice_in_dim(cells, 0, width, axis=dim)
        tail = lax.slice_in_dim(cells, cells.shape[dim] - width, cells.shape[dim], axis=dim)
        cells = jnp.concatenate(
            [
                lax.ppermute(tail, axis, [(i, (i + 1) % count) for i in range(ends)]),
                cells,
                lax.ppermute(head, axis, [((i + 1) % count, i) for i in range(ends)]),
            ],
            axis=dim,
        )
    return cells


def neighbours(field):
    return [
        field[2:, 1:-1, 1:-1],
        field[:-2, 1:-1, 1:-1],
        field[1:-1, 2:, 1:-1],
        field[1:-1, :-2, 1:-1],
        field[1:-1, 1:-1, 2:],
        field[1:-1, 1:-1, :-2],
    ]


def apply_stencil(field, coefs):
    middle = field[1:-1, 1:-1, 1:-1]
    centre_coef = coefs[1:-1, 1:-1, 1:-1]
    accumulated = jnp.zeros_like(middle)
    for beside, other in zip(neighbours(field), neighbours(coefs)):
        other = jnp.where(other > 0, other, centre_coef)
        accumulated = accumulated + 0.5 * (centre_coef + other) * (middle - beside)
    return accumulated


def edge_rims(widened, planes_here, margin):
    first = widened[..., :margin]
    last = lax.dynamic_slice_in_dim(widened, planes_here - margin, margin, axis=widened.ndim - 1)
    return jnp.concatenate([first, last], axis=-1)


def stitch(widened, rims, planes_here, margin):
    before = rims[..., :margin]
    after = rims[..., 3 * margin :]
    buffer = jnp.concatenate([before, widened, jnp.zeros_like(before)], axis=-1)
    return lax.dynamic_update_slice_in_dim(
        buffer, after, planes_here + margin, axis=buffer.ndim - 1
    )


def on_device(right_side, coefficient, start_vector, plane_counts):
    slots = right_side.shape[2]
    planes_here = lax.dynamic_index_in_dim(plane_counts, lax.axis_index("gz"), 0, keepdims=False)
    alive_mask = lax.broadcasted_iota(jnp.int32, (1, 1, slots), 2) < planes_here
    rhs = jnp.where(alive_mask, right_side, 0.0)
    coefs = jnp.where(alive_mask, coefficient, 0.0)
    start = jnp.where(alive_mask, start_vector, 0.0)
    reach = 1
    coef_wide = padded(coefs, (("gx", 0), ("gy", 1)), reach)
    coef_rims = padded(edge_rims(coef_wide, planes_here, reach), (("gz", 2),), reach)
    weights_full = stitch(coef_wide, coef_rims, planes_here, reach)

    def single(field):
        widened = padded(field, (("gx", 0), ("gy", 1)), 1)
        rims = padded(edge_rims(widened, planes_here, 1), (("gz", 2),), 1)
        return jnp.where(
            alive_mask, apply_stencil(stitch(widened, rims, planes_here, 1), weights_full), 0.0
        )

    vector = start
    previous = start
    for sweep in range(POWER):
        previous = vector
        vector = single(vector)
    upper_sum, lower_sum = lax.psum(
        (jnp.sum(vector * vector), jnp.sum(previous * previous)), ("gx", "gy", "gz")
    )
    largest = jnp.sqrt(upper_sum / lower_sum)
    center = 0.6 * largest
    half_width = 0.5 * largest
    sharpness = 1.2
    ratio = 1.0 / sharpness
    solution = jnp.zeros_like(rhs)
    residue = rhs
    direction = rhs / center
    for section in range(DEGREE):
        solution = solution + direction
        residue = residue - single(direction)
        if section < DEGREE - 1:
            fresh = 1.0 / (2.0 * sharpness - ratio)
            direction = fresh * ratio * direction + 2.0 * fresh / half_width * residue
            ratio = fresh
    return (solution, residue)


def solution(mesh):
    in_specs = (P("gx", "gy", "gz"), P("gx", "gy", "gz"), P("gx", "gy", "gz"), P())
    out_specs = (P("gx", "gy", "gz"), P("gx", "gy", "gz"))
    return jax.shard_map(
        on_device, mesh=mesh, in_specs=in_specs, out_specs=out_specs, check_vma=False
    )
```

profile of v0, /device:TPU:1, one launch (start us, length us, event | category | flops | bytes accessed | tf_op | source)
XLA Modules:
  0.0 258.0 jit_solution(11213246677798862523)
XLA Ops:
  3.5 4.0 %collective-permute-start = (f32[1,16,128]{2,1,0:T(8,128)S(1)}, f32[1,16,128]{2,1,0:T(8,128)S(1)}, u32[]{:S(2)}, u32[]{:S(2)}) collective-permute-start(f32[1,16,128]{2,1,0:T(8,128)S(1)} %get-tuple-element.65), channel_id=1, source_target_pairs={{0,16},{1,17},{2,18},{3,19},{4,20},{5,21},{6,22},{7,23},{8,24},{9,... | collective-permute-start | bytes 24584 | tf_op jit(solution)/shard_map/ppermute | solution.py:18
  8.8 4.0 %collective-permute-start.6 = (f32[1,16,128]{2,1,0:T(8,128)S(1)}, f32[1,16,128]{2,1,0:T(8,128)S(1)}, u32[]{:S(2)}, u32[]{:S(2)}) collective-permute-start(f32[1,16,128]{2,1,0:T(8,128)S(1)} %get-tuple-element.67), channel_id=1, source_target_pairs={{0,16},{1,17},{2,18},{3,19},{4,20},{5,21},{6,22},{7,23},{8,24},{9,... | collective-permute-start | bytes 24584 | tf_op jit(solution)/shard_map/ppermute | solution.py:18
  15.4 3.2 %collective-permute-start.2 = (f32[18,1,128]{2,1,0:T(1,128)S(1)}, f32[18,1,128]{2,1,0:T(1,128)S(1)}, u32[]{:S(2)}, u32[]{:S(2)}) collective-permute-start(f32[18,1,128]{2,1,0:T(1,128)S(1)} %get-tuple-element.47), channel_id=1, source_target_pairs={{0,4},{4,8},{8,12},{1,5},{5,9},{9,13},{2,6},{6,10},{10,14},{3,7},{... | collective-permute-start | bytes 27656 | tf_op jit(solution)/shard_map/ppermute | solution.py:18
  20.0 4.0 %collective-permute-start.8 = (f32[18,1,128]{2,1,0:T(1,128)S(1)}, f32[18,1,128]{2,1,0:T(1,128)S(1)}, u32[]{:S(2)}, u32[]{:S(2)}) collective-permute-start(f32[18,1,128]{2,1,0:T(1,128)S(1)} %get-tuple-element.49), channel_id=1, source_target_pairs={{0,4},{4,8},{8,12},{1,5},{5,9},{9,13},{2,6},{6,10},{10,14},{3,7},{... | collective-permute-start | bytes 27656 | tf_op jit(solution)/shard_map/ppermute | solution.py:18
  25.5 2.9 %collective-permute-done.9 = f32[18,1,128]{2,1,0:T(1,128)S(1)} collective-permute-done((f32[18,1,128]{2,1,0:T(1,128)S(1)}, f32[18,1,128]{2,1,0:T(1,128)S(1)}, u32[]{:S(2)}, u32[]{:S(2)}) %collective-permute-start.9) | collective-permute-done | bytes 9248 | tf_op jit(solution)/shard_map/ppermute | solution.py:20
  28.6 6.5 %collective-permute-start.10 = (f32[18,18,1]{2,1,0:T(8,128)S(1)}, f32[18,18,1]{2,1,0:T(8,128)S(1)}, u32[]{:S(2)}, u32[]{:S(2)}) collective-permute-start(f32[18,18,1]{2,1,0:T(8,128)S(1)} %get-tuple-element.34), channel_id=1, source_target_pairs={{0,1},{1,2},{2,3},{4,5},{5,6},{6,7},{8,9},{9,10},{10,11},{12,13},{... | collective-permute-start | bytes 3896 | tf_op jit(solution)/shard_map/ppermute | solution.py:18
  35.1 1.9 collective-permute-start.4
  38.4 2.4 collective-permute-start.11
  40.8 1.9 collective-permute-start.5
  43.2 4.8 %collective-permute-done.5 = f32[18,18,1]{2,1,0:T(8,128)S(1)} collective-permute-done((f32[18,18,1]{2,1,0:T(8,128)S(1)}, f32[18,18,1]{2,1,0:T(8,128)S(1)}, u32[]{:S(2)}, u32[]{:S(2)}) %collective-permute-start.5) | collective-permute-done | bytes 1328 | tf_op jit(solution)/shard_map/ppermute | solution.py:20
  48.0 1.4 dynamic_update_slice.24
  49.5 1.4 dynamic_update_slice.25
  51.4 4.3 %collective-permute-start.12 = (f32[1,16,128]{2,1,0:T(8,128)S(1)}, f32[1,16,128]{2,1,0:T(8,128)S(1)}, u32[]{:S(2)}, u32[]{:S(2)}) collective-permute-start(f32[1,16,128]{2,1,0:T(8,128)S(1)} %get-tuple-element.63), channel_id=1, source_target_pairs={{0,16},{1,17},{2,18},{3,19},{4,20},{5,21},{6,22},{7,23},{8,24},{9,... | collective-permute-start | bytes 24584 | tf_op jit(solution)/shard_map/ppermute | solution.py:18
  55.7 1.3 collective-permute-start.13
  57.0 3.1 %collective-permute-done.13 = f32[1,16,128]{2,1,0:T(8,128)S(1)} collective-permute-done((f32[1,16,128]{2,1,0:T(8,128)S(1)}, f32[1,16,128]{2,1,0:T(8,128)S(1)}, u32[]{:S(2)}, u32[]{:S(2)}) %collective-permute-start.13) | collective-permute-done | bytes 8224 | tf_op jit(solution)/shard_map/ppermute | solution.py:20
  60.1 3.2 %collective-permute-start.14 = (f32[18,1,128]{2,1,0:T(1,128)S(1)}, f32[18,1,128]{2,1,0:T(1,128)S(1)}, u32[]{:S(2)}, u32[]{:S(2)}) collective-permute-start(f32[18,1,128]{2,1,0:T(1,128)S(1)} %get-tuple-element.45), channel_id=1, source_target_pairs={{0,4},{4,8},{8,12},{1,5},{5,9},{9,13},{2,6},{6,10},{10,14},{3,7},{... | collective-permute-start | bytes 27656 | tf_op jit(solution)/shard_map/ppermute | solution.py:18
  63.3 1.3 collective-permute-start.15
  64.6 3.1 %collective-permute-done.15 = f32[18,1,128]{2,1,0:T(1,128)S(1)} collective-permute-done((f32[18,1,128]{2,1,0:T(1,128)S(1)}, f32[18,1,128]{2,1,0:T(1,128)S(1)}, u32[]{:S(2)}, u32[]{:S(2)}) %collective-permute-start.15) | collective-permute-done | bytes 9248 | tf_op jit(solution)/shard_map/ppermute | solution.py:20
  67.9 4.6 %collective-permute-start.16 = (f32[18,18,1]{2,1,0:T(8,128)S(1)}, f32[18,18,1]{2,1,0:T(8,128)S(1)}, u32[]{:S(2)}, u32[]{:S(2)}) collective-permute-start(f32[18,18,1]{2,1,0:T(8,128)S(1)} %get-tuple-element.30), channel_id=1, source_target_pairs={{0,1},{1,2},{2,3},{4,5},{5,6},{6,7},{8,9},{9,10},{10,11},{12,13},{... | collective-permute-start | bytes 3896 | tf_op jit(solution)/shard_map/ppermute | solution.py:18
  72.5 1.9 collective-permute-start.17
  75.6 4.1 %collective-permute-done.17 = f32[18,18,1]{2,1,0:T(8,128)S(1)} collective-permute-done((f32[18,18,1]{2,1,0:T(8,128)S(1)}, f32[18,18,1]{2,1,0:T(8,128)S(1)}, u32[]{:S(2)}, u32[]{:S(2)}) %collective-permute-start.17) | collective-permute-done | bytes 1328 | tf_op jit(solution)/shard_map/ppermute | solution.py:20
  79.8 1.4 dynamic_update_slice.26
  82.1 1.4 collective-permute-start.18
  83.4 1.3 collective-permute-start.19
  84.8 3.1 %collective-permute-done.19 = f32[1,16,128]{2,1,0:T(8,128)S(1)} collective-permute-done((f32[1,16,128]{2,1,0:T(8,128)S(1)}, f32[1,16,128]{2,1,0:T(8,128)S(1)}, u32[]{:S(2)}, u32[]{:S(2)}) %collective-permute-start.19) | collective-permute-done | bytes 8224 | tf_op jit(solution)/shard_map/ppermute | solution.py:20
  87.9 3.2 %collective-permute-start.20 = (f32[18,1,128]{2,1,0:T(1,128)S(1)}, f32[18,1,128]{2,1,0:T(1,128)S(1)}, u32[]{:S(2)}, u32[]{:S(2)}) collective-permute-start(f32[18,1,128]{2,1,0:T(1,128)S(1)} %get-tuple-element.43), channel_id=1, source_target_pairs={{0,4},{4,8},{8,12},{1,5},{5,9},{9,13},{2,6},{6,10},{10,14},{3,7},{... | collective-permute-start | bytes 27656 | tf_op jit(solution)/shard_map/ppermute | solution.py:18
  92.4 3.1 %collective-permute-done.21 = f32[18,1,128]{2,1,0:T(1,128)S(1)} collective-permute-done((f32[18,1,128]{2,1,0:T(1,128)S(1)}, f32[18,1,128]{2,1,0:T(1,128)S(1)}, u32[]{:S(2)}, u32[]{:S(2)}) %collective-permute-start.21) | collective-permute-done | bytes 9248 | tf_op jit(solution)/shard_map/ppermute | solution.py:20
  95.6 4.6 %collective-permute-start.22 = (f32[18,18,1]{2,1,0:T(8,128)S(1)}, f32[18,18,1]{2,1,0:T(8,128)S(1)}, u32[]{:S(2)}, u32[]{:S(2)}) collective-permute-start(f32[18,18,1]{2,1,0:T(8,128)S(1)} %get-tuple-element.28), channel_id=1, source_target_pairs={{0,1},{1,2},{2,3},{4,5},{5,6},{6,7},{8,9},{9,10},{10,11},{12,13},{... | collective-permute-start | bytes 3896 | tf_op jit(solution)/shard_map/ppermute | solution.py:18
  100.3 1.9 collective-permute-start.23
  103.4 4.1 %collective-permute-done.23 = f32[18,18,1]{2,1,0:T(8,128)S(1)} collective-permute-done((f32[18,18,1]{2,1,0:T(8,128)S(1)}, f32[18,18,1]{2,1,0:T(8,128)S(1)}, u32[]{:S(2)}, u32[]{:S(2)}) %collective-permute-start.23) | collective-permute-done | bytes 1328 | tf_op jit(solution)/shard_map/ppermute | solution.py:20
  107.5 1.4 dynamic_update_slice.27
  109.8 35.2 %all-reduce = (f32[]{:T(128)}, f32[]{:T(128)}) all-reduce(f32[]{:T(128)} %fusion.68, f32[]{:T(128)} %get-tuple-element.10), channel_id=1, replica_groups=mesh['gx'=2,'gy'=4,'gz'=4] {'gx','gy','gz'}, use_global_device_ids=true, to_apply=%region_1.2 | all-reduce | flops 2 | bytes 16 | tf_op jit(solution)/shard_map/psum | solution.py:87
  146.5 4.3 %collective-permute-start.24 = (f32[1,16,128]{2,1,0:T(8,128)S(1)}, f32[1,16,128]{2,1,0:T(8,128)S(1)}, u32[]{:S(2)}, u32[]{:S(2)}) collective-permute-start(f32[1,16,128]{2,1,0:T(8,128)S(1)} %get-tuple-element.59), channel_id=1, source_target_pairs={{0,16},{1,17},{2,18},{3,19},{4,20},{5,21},{6,22},{7,23},{8,24},{9,... | collective-permute-start | bytes 24584 | tf_op jit(solution)/shard_map/ppermute | solution.py:18
  152.2 3.1 %collective-permute-done.25 = f32[1,16,128]{2,1,0:T(8,128)S(1)} collective-permute-done((f32[1,16,128]{2,1,0:T(8,128)S(1)}, f32[1,16,128]{2,1,0:T(8,128)S(1)}, u32[]{:S(2)}, u32[]{:S(2)}) %collective-permute-start.25) | collective-permute-done | bytes 8224 | tf_op jit(solution)/shard_map/ppermute | solution.py:20
  155.3 3.6 %collective-permute-start.26 = (f32[18,1,128]{2,1,0:T(1,128)S(1)}, f32[18,1,128]{2,1,0:T(1,128)S(1)}, u32[]{:S(2)}, u32[]{:S(2)}) collective-permute-start(f32[18,1,128]{2,1,0:T(1,128)S(1)} %get-tuple-element.41), channel_id=1, source_target_pairs={{0,4},{4,8},{8,12},{1,5},{5,9},{9,13},{2,6},{6,10},{10,14},{3,7},{... | collective-permute-start | bytes 27656 | tf_op jit(solution)/shard_map/ppermute | solution.py:18
  160.2 3.1 %collective-permute-done.27 = f32[18,1,128]{2,1,0:T(1,128)S(1)} collective-permute-done((f32[18,1,128]{2,1,0:T(1,128)S(1)}, f32[18,1,128]{2,1,0:T(1,128)S(1)}, u32[]{:S(2)}, u32[]{:S(2)}) %collective-permute-start.27) | collective-permute-done | bytes 9248 | tf_op jit(solution)/shard_map/ppermute | solution.py:20
  163.5 7.3 %collective-permute-start.28 = (f32[18,18,1]{2,1,0:T(8,128)S(1)}, f32[18,18,1]{2,1,0:T(8,128)S(1)}, u32[]{:S(2)}, u32[]{:S(2)}) collective-permute-start(f32[18,18,1]{2,1,0:T(8,128)S(1)} %get-tuple-element.26), channel_id=1, source_target_pairs={{0,1},{1,2},{2,3},{4,5},{5,6},{6,7},{8,9},{9,10},{10,11},{12,13},{... | collective-permute-start | bytes 3896 | tf_op jit(solution)/shard_map/ppermute | solution.py:18
  170.8 1.9 collective-permute-start.29
  173.9 4.2 %collective-permute-done.29 = f32[18,18,1]{2,1,0:T(8,128)S(1)} collective-permute-done((f32[18,18,1]{2,1,0:T(8,128)S(1)}, f32[18,18,1]{2,1,0:T(8,128)S(1)}, u32[]{:S(2)}, u32[]{:S(2)}) %collective-permute-start.29) | collective-permute-done | bytes 1328 | tf_op jit(solution)/shard_map/ppermute | solution.py:20
  178.1 1.4 dynamic_update_slice.28
  179.8 1.4 collective-permute-start.30
  182.5 3.1 %collective-permute-done.31 = f32[1,16,128]{2,1,0:T(8,128)S(1)} collective-permute-done((f32[1,16,128]{2,1,0:T(8,128)S(1)}, f32[1,16,128]{2,1,0:T(8,128)S(1)}, u32[]{:S(2)}, u32[]{:S(2)}) %collective-permute-start.31) | collective-permute-done | bytes 8224 | tf_op jit(solution)/shard_map/ppermute | solution.py:20
  185.6 2.3 collective-permute-start.32
  189.2 3.1 %collective-permute-done.33 = f32[18,1,128]{2,1,0:T(1,128)S(1)} collective-permute-done((f32[18,1,128]{2,1,0:T(1,128)S(1)}, f32[18,1,128]{2,1,0:T(1,128)S(1)}, u32[]{:S(2)}, u32[]{:S(2)}) %collective-permute-start.33) | collective-permute-done | bytes 9248 | tf_op jit(solution)/shard_map/ppermute | solution.py:20
  192.5 4.6 %collective-permute-start.34 = (f32[18,18,1]{2,1,0:T(8,128)S(1)}, f32[18,18,1]{2,1,0:T(8,128)S(1)}, u32[]{:S(2)}, u32[]{:S(2)}) collective-permute-start(f32[18,18,1]{2,1,0:T(8,128)S(1)} %get-tuple-element.24), channel_id=1, source_target_pairs={{0,1},{1,2},{2,3},{4,5},{5,6},{6,7},{8,9},{9,10},{10,11},{12,13},{... | collective-permute-start | bytes 3896 | tf_op jit(solution)/shard_map/ppermute | solution.py:18
  197.1 1.9 collective-permute-start.35
  200.2 4.2 %collective-permute-done.35 = f32[18,18,1]{2,1,0:T(8,128)S(1)} collective-permute-done((f32[18,18,1]{2,1,0:T(8,128)S(1)}, f32[18,18,1]{2,1,0:T(8,128)S(1)}, u32[]{:S(2)}, u32[]{:S(2)}) %collective-permute-start.35) | collective-permute-done | bytes 1328 | tf_op jit(solution)/shard_map/ppermute | solution.py:20
  204.4 1.4 dynamic_update_slice.29
  206.1 1.4 collective-permute-start.36
  208.8 3.1 %collective-permute-done.37 = f32[1,16,128]{2,1,0:T(8,128)S(1)} collective-permute-done((f32[1,16,128]{2,1,0:T(8,128)S(1)}, f32[1,16,128]{2,1,0:T(8,128)S(1)}, u32[]{:S(2)}, u32[]{:S(2)}) %collective-permute-start.37) | collective-permute-done | bytes 8224 | tf_op jit(solution)/shard_map/ppermute | solution.py:20
  211.9 1.6 collective-permute-start.38
  214.9 3.1 %collective-permute-done.39 = f32[18,1,128]{2,1,0:T(1,128)S(1)} collective-permute-done((f32[18,1,128]{2,1,0:T(1,128)S(1)}, f32[18,1,128]{2,1,0:T(1,128)S(1)}, u32[]{:S(2)}, u32[]{:S(2)}) %collective-permute-start.39) | collective-permute-done | bytes 9248 | tf_op jit(solution)/shard_map/ppermute | solution.py:20
  218.1 4.6 %collective-permute-start.40 = (f32[18,18,1]{2,1,0:T(8,128)S(1)}, f32[18,18,1]{2,1,0:T(8,128)S(1)}, u32[]{:S(2)}, u32[]{:S(2)}) collective-permute-start(f32[18,18,1]{2,1,0:T(8,128)S(1)} %get-tuple-element.22), channel_id=1, source_target_pairs={{0,1},{1,2},{2,3},{4,5},{5,6},{6,7},{8,9},{9,10},{10,11},{12,13},{... | collective-permute-start | bytes 3896 | tf_op jit(solution)/shard_map/ppermute | solution.py:18
  222.8 1.9 collective-permute-start.41
  225.9 4.2 %collective-permute-done.41 = f32[18,18,1]{2,1,0:T(8,128)S(1)} collective-permute-done((f32[18,18,1]{2,1,0:T(8,128)S(1)}, f32[18,18,1]{2,1,0:T(8,128)S(1)}, u32[]{:S(2)}, u32[]{:S(2)}) %collective-permute-start.41) | collective-permute-done | bytes 1328 | tf_op jit(solution)/shard_map/ppermute | solution.py:20
  230.0 1.4 dynamic_update_slice.30
  231.8 1.4 collective-permute-start.42
  234.4 3.1 %collective-permute-done.43 = f32[1,16,128]{2,1,0:T(8,128)S(1)} collective-permute-done((f32[1,16,128]{2,1,0:T(8,128)S(1)}, f32[1,16,128]{2,1,0:T(8,128)S(1)}, u32[]{:S(2)}, u32[]{:S(2)}) %collective-permute-start.43) | collective-permute-done | bytes 8224 | tf_op jit(solution)/shard_map/ppermute | solution.py:20
  237.5 1.6 collective-permute-start.44
  240.5 3.1 %collective-permute-done.45 = f32[18,1,128]{2,1,0:T(1,128)S(1)} collective-permute-done((f32[18,1,128]{2,1,0:T(1,128)S(1)}, f32[18,1,128]{2,1,0:T(1,128)S(1)}, u32[]{:S(2)}, u32[]{:S(2)}) %collective-permute-start.45) | collective-permute-done | bytes 9248 | tf_op jit(solution)/shard_map/ppermute | solution.py:20
  243.8 4.6 %collective-permute-start.46 = (f32[18,18,1]{2,1,0:T(8,128)S(1)}, f32[18,18,1]{2,1,0:T(8,128)S(1)}, u32[]{:S(2)}, u32[]{:S(2)}) collective-permute-start(f32[18,18,1]{2,1,0:T(8,128)S(1)} %get-tuple-element.20), channel_id=1, source_target_pairs={{0,1},{1,2},{2,3},{4,5},{5,6},{6,7},{8,9},{9,10},{10,11},{12,13},{... | collective-permute-start | bytes 3896 | tf_op jit(solution)/shard_map/ppermute | solution.py:18
  248.4 1.9 collective-permute-start.47
  251.5 4.1 %collective-permute-done.47 = f32[18,18,1]{2,1,0:T(8,128)S(1)} collective-permute-done((f32[18,18,1]{2,1,0:T(8,128)S(1)}, f32[18,18,1]{2,1,0:T(8,128)S(1)}, u32[]{:S(2)}, u32[]{:S(2)}) %collective-permute-start.47) | collective-permute-done | bytes 1328 | tf_op jit(solution)/shard_map/ppermute | solution.py:20
  255.6 1.4 dynamic_update_slice.31
  (96 shorter events, 32.7 us)
Async XLA Ops:
  0.6 0.7 copy-start.1
  3.5 11.9 %collective-permute-start = (f32[1,16,128]{2,1,0:T(8,128)S(1)}, f32[1,16,128]{2,1,0:T(8,128)S(1)}, u32[]{:S(2)}, u32[]{:S(2)}) collective-permute-start(f32[1,16,128]{2,1,0:T(8,128)S(1)} %get-tuple-element.65), channel_id=1, source_target_pairs={{0,16},{1,17},{2,18},{3,19},{4,20},{5,21},{6,22},{7,23},{8,24},{9,... | collective-permute-start | bytes 24584 | tf_op jit(solution)/shard_map/ppermute | solution.py:18
  7.5 7.9 %collective-permute-start.1 = (f32[1,16,128]{2,1,0:T(8,128)S(1)}, f32[1,16,128]{2,1,0:T(8,128)S(1)}, u32[]{:S(2)}, u32[]{:S(2)}) collective-permute-start(f32[1,16,128]{2,1,0:T(8,128)S(1)} %get-tuple-element.66), channel_id=1, source_target_pairs={{16,0},{17,1},{18,2},{19,3},{20,4},{21,5},{22,6},{23,7},{24,8},{25... | collective-permute-start | bytes 24584 | tf_op jit(solution)/shard_map/ppermute | solution.py:20
  8.8 11.1 %collective-permute-start.6 = (f32[1,16,128]{2,1,0:T(8,128)S(1)}, f32[1,16,128]{2,1,0:T(8,128)S(1)}, u32[]{:S(2)}, u32[]{:S(2)}) collective-permute-start(f32[1,16,128]{2,1,0:T(8,128)S(1)} %get-tuple-element.67), channel_id=1, source_target_pairs={{0,16},{1,17},{2,18},{3,19},{4,20},{5,21},{6,22},{7,23},{8,24},{9,... | collective-permute-start | bytes 24584 | tf_op jit(solution)/shard_map/ppermute | solution.py:18
  12.8 7.2 %collective-permute-start.7 = (f32[1,16,128]{2,1,0:T(8,128)S(1)}, f32[1,16,128]{2,1,0:T(8,128)S(1)}, u32[]{:S(2)}, u32[]{:S(2)}) collective-permute-start(f32[1,16,128]{2,1,0:T(8,128)S(1)} %get-tuple-element.68), channel_id=1, source_target_pairs={{16,0},{17,1},{18,2},{19,3},{20,4},{21,5},{22,6},{23,7},{24,8},{25... | collective-permute-start | bytes 24584 | tf_op jit(solution)/shard_map/ppermute | solution.py:20
  15.4 9.9 %collective-permute-start.2 = (f32[18,1,128]{2,1,0:T(1,128)S(1)}, f32[18,1,128]{2,1,0:T(1,128)S(1)}, u32[]{:S(2)}, u32[]{:S(2)}) collective-permute-start(f32[18,1,128]{2,1,0:T(1,128)S(1)} %get-tuple-element.47), channel_id=1, source_target_pairs={{0,4},{4,8},{8,12},{1,5},{5,9},{9,13},{2,6},{6,10},{10,14},{3,7},{... | collective-permute-start | bytes 27656 | tf_op jit(solution)/shard_map/ppermute | solution.py:18
  18.7 6.7 %collective-permute-start.3 = (f32[18,1,128]{2,1,0:T(1,128)S(1)}, f32[18,1,128]{2,1,0:T(1,128)S(1)}, u32[]{:S(2)}, u32[]{:S(2)}) collective-permute-start(f32[18,1,128]{2,1,0:T(1,128)S(1)} %get-tuple-element.48), channel_id=1, source_target_pairs={{4,0},{8,4},{12,8},{5,1},{9,5},{13,9},{6,2},{10,6},{14,10},{7,3},{... | collective-permute-start | bytes 27656 | tf_op jit(solution)/shard_map/ppermute | solution.py:20
  20.0 5.5 %collective-permute-start.8 = (f32[18,1,128]{2,1,0:T(1,128)S(1)}, f32[18,1,128]{2,1,0:T(1,128)S(1)}, u32[]{:S(2)}, u32[]{:S(2)}) collective-permute-start(f32[18,1,128]{2,1,0:T(1,128)S(1)} %get-tuple-element.49), channel_id=1, source_target_pairs={{0,4},{4,8},{8,12},{1,5},{5,9},{9,13},{2,6},{6,10},{10,14},{3,7},{... | collective-permute-start | bytes 27656 | tf_op jit(solution)/shard_map/ppermute | solution.py:18
  24.0 4.4 %collective-permute-start.9 = (f32[18,1,128]{2,1,0:T(1,128)S(1)}, f32[18,1,128]{2,1,0:T(1,128)S(1)}, u32[]{:S(2)}, u32[]{:S(2)}) collective-permute-start(f32[18,1,128]{2,1,0:T(1,128)S(1)} %get-tuple-element.50), channel_id=1, source_target_pairs={{4,0},{8,4},{12,8},{5,1},{9,5},{13,9},{6,2},{10,6},{14,10},{7,3},{... | collective-permute-start | bytes 27656 | tf_op jit(solution)/shard_map/ppermute | solution.py:20
  28.6 14.2 %collective-permute-start.10 = (f32[18,18,1]{2,1,0:T(8,128)S(1)}, f32[18,18,1]{2,1,0:T(8,128)S(1)}, u32[]{:S(2)}, u32[]{:S(2)}) collective-permute-start(f32[18,18,1]{2,1,0:T(8,128)S(1)} %get-tuple-element.34), channel_id=1, source_target_pairs={{0,1},{1,2},{2,3},{4,5},{5,6},{6,7},{8,9},{9,10},{10,11},{12,13},{... | collective-permute-start | bytes 3896 | tf_op jit(solution)/shard_map/ppermute | solution.py:18
  35.1 7.7 %collective-permute-start.4 = (f32[18,18,1]{2,1,0:T(8,128)S(1)}, f32[18,18,1]{2,1,0:T(8,128)S(1)}, u32[]{:S(2)}, u32[]{:S(2)}) collective-permute-start(f32[18,18,1]{2,1,0:T(8,128)S(1)} %get-tuple-element.32), channel_id=1, source_target_pairs={{0,1},{1,2},{2,3},{4,5},{5,6},{6,7},{8,9},{9,10},{10,11},{12,13},{... | collective-permute-start | bytes 3896 | tf_op jit(solution)/shard_map/ppermute | solution.py:18
  38.4 11.1 %collective-permute-start.11 = (f32[18,18,1]{2,1,0:T(8,128)S(1)}, f32[18,18,1]{2,1,0:T(8,128)S(1)}, u32[]{:S(2)}, u32[]{:S(2)}) collective-permute-start(f32[18,18,1]{2,1,0:T(8,128)S(1)} %get-tuple-element.33), channel_id=1, source_target_pairs={{1,0},{2,1},{3,2},{5,4},{6,5},{7,6},{9,8},{10,9},{11,10},{13,12},{... | collective-permute-start | bytes 3896 | tf_op jit(solution)/shard_map/ppermute | solution.py:20
  40.8 7.3 %collective-permute-start.5 = (f32[18,18,1]{2,1,0:T(8,128)S(1)}, f32[18,18,1]{2,1,0:T(8,128)S(1)}, u32[]{:S(2)}, u32[]{:S(2)}) collective-permute-start(f32[18,18,1]{2,1,0:T(8,128)S(1)} %get-tuple-element.31), channel_id=1, source_target_pairs={{1,0},{2,1},{3,2},{5,4},{6,5},{7,6},{9,8},{10,9},{11,10},{13,12},{... | collective-permute-start | bytes 3896 | tf_op jit(solution)/shard_map/ppermute | solution.py:20
  51.4 5.6 %collective-permute-start.12 = (f32[1,16,128]{2,1,0:T(8,128)S(1)}, f32[1,16,128]{2,1,0:T(8,128)S(1)}, u32[]{:S(2)}, u32[]{:S(2)}) collective-permute-start(f32[1,16,128]{2,1,0:T(8,128)S(1)} %get-tuple-element.63), channel_id=1, source_target_pairs={{0,16},{1,17},{2,18},{3,19},{4,20},{5,21},{6,22},{7,23},{8,24},{9,... | collective-permute-start | bytes 24584 | tf_op jit(solution)/shard_map/ppermute | solution.py:18
  55.7 4.4 %collective-permute-start.13 = (f32[1,16,128]{2,1,0:T(8,128)S(1)}, f32[1,16,128]{2,1,0:T(8,128)S(1)}, u32[]{:S(2)}, u32[]{:S(2)}) collective-permute-start(f32[1,16,128]{2,1,0:T(8,128)S(1)} %get-tuple-element.64), channel_id=1, source_target_pairs={{16,0},{17,1},{18,2},{19,3},{20,4},{21,5},{22,6},{23,7},{24,8},{25... | collective-permute-start | bytes 24584 | tf_op jit(solution)/shard_map/ppermute | solution.py:20
  60.1 4.5 %collective-permute-start.14 = (f32[18,1,128]{2,1,0:T(1,128)S(1)}, f32[18,1,128]{2,1,0:T(1,128)S(1)}, u32[]{:S(2)}, u32[]{:S(2)}) collective-permute-start(f32[18,1,128]{2,1,0:T(1,128)S(1)} %get-tuple-element.45), channel_id=1, source_target_pairs={{0,4},{4,8},{8,12},{1,5},{5,9},{9,13},{2,6},{6,10},{10,14},{3,7},{... | collective-permute-start | bytes 27656 | tf_op jit(solution)/shard_map/ppermute | solution.py:18
  63.3 4.4 %collective-permute-start.15 = (f32[18,1,128]{2,1,0:T(1,128)S(1)}, f32[18,1,128]{2,1,0:T(1,128)S(1)}, u32[]{:S(2)}, u32[]{:S(2)}) collective-permute-start(f32[18,1,128]{2,1,0:T(1,128)S(1)} %get-tuple-element.46), channel_id=1, source_target_pairs={{4,0},{8,4},{12,8},{5,1},{9,5},{13,9},{6,2},{10,6},{14,10},{7,3},{... | collective-permute-start | bytes 27656 | tf_op jit(solution)/shard_map/ppermute | solution.py:20
  67.9 7.5 %collective-permute-start.16 = (f32[18,18,1]{2,1,0:T(8,128)S(1)}, f32[18,18,1]{2,1,0:T(8,128)S(1)}, u32[]{:S(2)}, u32[]{:S(2)}) collective-permute-start(f32[18,18,1]{2,1,0:T(8,128)S(1)} %get-tuple-element.30), channel_id=1, source_target_pairs={{0,1},{1,2},{2,3},{4,5},{5,6},{6,7},{8,9},{9,10},{10,11},{12,13},{... | collective-permute-start | bytes 3896 | tf_op jit(solution)/shard_map/ppermute | solution.py:18
  72.5 7.3 %collective-permute-start.17 = (f32[18,18,1]{2,1,0:T(8,128)S(1)}, f32[18,18,1]{2,1,0:T(8,128)S(1)}, u32[]{:S(2)}, u32[]{:S(2)}) collective-permute-start(f32[18,18,1]{2,1,0:T(8,128)S(1)} %get-tuple-element.29), channel_id=1, source_target_pairs={{1,0},{2,1},{3,2},{5,4},{6,5},{7,6},{9,8},{10,9},{11,10},{13,12},{... | collective-permute-start | bytes 3896 | tf_op jit(solution)/shard_map/ppermute | solution.py:20
  82.1 2.7 %collective-permute-start.18 = (f32[1,16,128]{2,1,0:T(8,128)S(1)}, f32[1,16,128]{2,1,0:T(8,128)S(1)}, u32[]{:S(2)}, u32[]{:S(2)}) collective-permute-start(f32[1,16,128]{2,1,0:T(8,128)S(1)} %get-tuple-element.61), channel_id=1, source_target_pairs={{0,16},{1,17},{2,18},{3,19},{4,20},{5,21},{6,22},{7,23},{8,24},{9,... | collective-permute-start | bytes 24584 | tf_op jit(solution)/shard_map/ppermute | solution.py:18
  83.4 4.4 %collective-permute-start.19 = (f32[1,16,128]{2,1,0:T(8,128)S(1)}, f32[1,16,128]{2,1,0:T(8,128)S(1)}, u32[]{:S(2)}, u32[]{:S(2)}) collective-permute-start(f32[1,16,128]{2,1,0:T(8,128)S(1)} %get-tuple-element.62), channel_id=1, source_target_pairs={{16,0},{17,1},{18,2},{19,3},{20,4},{21,5},{22,6},{23,7},{24,8},{25... | collective-permute-start | bytes 24584 | tf_op jit(solution)/shard_map/ppermute | solution.py:20
  87.9 4.5 %collective-permute-start.20 = (f32[18,1,128]{2,1,0:T(1,128)S(1)}, f32[18,1,128]{2,1,0:T(1,128)S(1)}, u32[]{:S(2)}, u32[]{:S(2)}) collective-permute-start(f32[18,1,128]{2,1,0:T(1,128)S(1)} %get-tuple-element.43), channel_id=1, source_target_pairs={{0,4},{4,8},{8,12},{1,5},{5,9},{9,13},{2,6},{6,10},{10,14},{3,7},{... | collective-permute-start | bytes 27656 | tf_op jit(solution)/shard_map/ppermute | solution.py:18
  91.1 4.4 %collective-permute-start.21 = (f32[18,1,128]{2,1,0:T(1,128)S(1)}, f32[18,1,128]{2,1,0:T(1,128)S(1)}, u32[]{:S(2)}, u32[]{:S(2)}) collective-permute-start(f32[18,1,128]{2,1,0:T(1,128)S(1)} %get-tuple-element.44), channel_id=1, source_target_pairs={{4,0},{8,4},{12,8},{5,1},{9,5},{13,9},{6,2},{10,6},{14,10},{7,3},{... | collective-permute-start | bytes 27656 | tf_op jit(solution)/shard_map/ppermute | solution.py:20
  95.6 7.5 %collective-permute-start.22 = (f32[18,18,1]{2,1,0:T(8,128)S(1)}, f32[18,18,1]{2,1,0:T(8,128)S(1)}, u32[]{:S(2)}, u32[]{:S(2)}) collective-permute-start(f32[18,18,1]{2,1,0:T(8,128)S(1)} %get-tuple-element.28), channel_id=1, source_target_pairs={{0,1},{1,2},{2,3},{4,5},{5,6},{6,7},{8,9},{9,10},{10,11},{12,13},{... | collective-permute-start | bytes 3896 | tf_op jit(solution)/shard_map/ppermute | solution.py:18
  100.3 7.3 %collective-permute-start.23 = (f32[18,18,1]{2,1,0:T(8,128)S(1)}, f32[18,18,1]{2,1,0:T(8,128)S(1)}, u32[]{:S(2)}, u32[]{:S(2)}) collective-permute-start(f32[18,18,1]{2,1,0:T(8,128)S(1)} %get-tuple-element.27), channel_id=1, source_target_pairs={{1,0},{2,1},{3,2},{5,4},{6,5},{7,6},{9,8},{10,9},{11,10},{13,12},{... | collective-permute-start | bytes 3896 | tf_op jit(solution)/shard_map/ppermute | solution.py:20
  108.9 37.5 %copy-start = (f32[16,16,128]{2,1,0:T(8,128)S(1)}, f32[16,16,128]{2,1,0:T(8,128)}, u32[]{:S(2)}) copy-start(f32[16,16,128]{2,1,0:T(8,128)} %param.4) | copy-start | bytes 393220
  146.5 5.7 %collective-permute-start.24 = (f32[1,16,128]{2,1,0:T(8,128)S(1)}, f32[1,16,128]{2,1,0:T(8,128)S(1)}, u32[]{:S(2)}, u32[]{:S(2)}) collective-permute-start(f32[1,16,128]{2,1,0:T(8,128)S(1)} %get-tuple-element.59), channel_id=1, source_target_pairs={{0,16},{1,17},{2,18},{3,19},{4,20},{5,21},{6,22},{7,23},{8,24},{9,... | collective-permute-start | bytes 24584 | tf_op jit(solution)/shard_map/ppermute | solution.py:18
  150.8 4.4 %collective-permute-start.25 = (f32[1,16,128]{2,1,0:T(8,128)S(1)}, f32[1,16,128]{2,1,0:T(8,128)S(1)}, u32[]{:S(2)}, u32[]{:S(2)}) collective-permute-start(f32[1,16,128]{2,1,0:T(8,128)S(1)} %get-tuple-element.60), channel_id=1, source_target_pairs={{16,0},{17,1},{18,2},{19,3},{20,4},{21,5},{22,6},{23,7},{24,8},{25... | collective-permute-start | bytes 24584 | tf_op jit(solution)/shard_map/ppermute | solution.py:20
  155.3 4.9 %collective-permute-start.26 = (f32[18,1,128]{2,1,0:T(1,128)S(1)}, f32[18,1,128]{2,1,0:T(1,128)S(1)}, u32[]{:S(2)}, u32[]{:S(2)}) collective-permute-start(f32[18,1,128]{2,1,0:T(1,128)S(1)} %get-tuple-element.41), channel_id=1, source_target_pairs={{0,4},{4,8},{8,12},{1,5},{5,9},{9,13},{2,6},{6,10},{10,14},{3,7},{... | collective-permute-start | bytes 27656 | tf_op jit(solution)/shard_map/ppermute | solution.py:18
  158.9 4.4 %collective-permute-start.27 = (f32[18,1,128]{2,1,0:T(1,128)S(1)}, f32[18,1,128]{2,1,0:T(1,128)S(1)}, u32[]{:S(2)}, u32[]{:S(2)}) collective-permute-start(f32[18,1,128]{2,1,0:T(1,128)S(1)} %get-tuple-element.42), channel_id=1, source_target_pairs={{4,0},{8,4},{12,8},{5,1},{9,5},{13,9},{6,2},{10,6},{14,10},{7,3},{... | collective-permute-start | bytes 27656 | tf_op jit(solution)/shard_map/ppermute | solution.py:20
  163.5 10.2 %collective-permute-start.28 = (f32[18,18,1]{2,1,0:T(8,128)S(1)}, f32[18,18,1]{2,1,0:T(8,128)S(1)}, u32[]{:S(2)}, u32[]{:S(2)}) collective-permute-start(f32[18,18,1]{2,1,0:T(8,128)S(1)} %get-tuple-element.26), channel_id=1, source_target_pairs={{0,1},{1,2},{2,3},{4,5},{5,6},{6,7},{8,9},{9,10},{10,11},{12,13},{... | collective-permute-start | bytes 3896 | tf_op jit(solution)/shard_map/ppermute | solution.py:18
  170.8 7.3 %collective-permute-start.29 = (f32[18,18,1]{2,1,0:T(8,128)S(1)}, f32[18,18,1]{2,1,0:T(8,128)S(1)}, u32[]{:S(2)}, u32[]{:S(2)}) collective-permute-start(f32[18,18,1]{2,1,0:T(8,128)S(1)} %get-tuple-element.25), channel_id=1, source_target_pairs={{1,0},{2,1},{3,2},{5,4},{6,5},{7,6},{9,8},{10,9},{11,10},{13,12},{... | collective-permute-start | bytes 3896 | tf_op jit(solution)/shard_map/ppermute | solution.py:20
  179.8 2.7 %collective-permute-start.30 = (f32[1,16,128]{2,1,0:T(8,128)S(1)}, f32[1,16,128]{2,1,0:T(8,128)S(1)}, u32[]{:S(2)}, u32[]{:S(2)}) collective-permute-start(f32[1,16,128]{2,1,0:T(8,128)S(1)} %get-tuple-element.57), channel_id=1, source_target_pairs={{0,16},{1,17},{2,18},{3,19},{4,20},{5,21},{6,22},{7,23},{8,24},{9,... | collective-permute-start | bytes 24584 | tf_op jit(solution)/shard_map/ppermute | solution.py:18
  181.2 4.4 %collective-permute-start.31 = (f32[1,16,128]{2,1,0:T(8,128)S(1)}, f32[1,16,128]{2,1,0:T(8,128)S(1)}, u32[]{:S(2)}, u32[]{:S(2)}) collective-permute-start(f32[1,16,128]{2,1,0:T(8,128)S(1)} %get-tuple-element.58), channel_id=1, source_target_pairs={{16,0},{17,1},{18,2},{19,3},{20,4},{21,5},{22,6},{23,7},{24,8},{25... | collective-permute-start | bytes 24584 | tf_op jit(solution)/shard_map/ppermute | solution.py:20
  185.6 3.6 %collective-permute-start.32 = (f32[18,1,128]{2,1,0:T(1,128)S(1)}, f32[18,1,128]{2,1,0:T(1,128)S(1)}, u32[]{:S(2)}, u32[]{:S(2)}) collective-permute-start(f32[18,1,128]{2,1,0:T(1,128)S(1)} %get-tuple-element.39), channel_id=1, source_target_pairs={{0,4},{4,8},{8,12},{1,5},{5,9},{9,13},{2,6},{6,10},{10,14},{3,7},{... | collective-permute-start | bytes 27656 | tf_op jit(solution)/shard_map/ppermute | solution.py:18
  187.9 4.4 %collective-permute-start.33 = (f32[18,1,128]{2,1,0:T(1,128)S(1)}, f32[18,1,128]{2,1,0:T(1,128)S(1)}, u32[]{:S(2)}, u32[]{:S(2)}) collective-permute-start(f32[18,1,128]{2,1,0:T(1,128)S(1)} %get-tuple-element.40), channel_id=1, source_target_pairs={{4,0},{8,4},{12,8},{5,1},{9,5},{13,9},{6,2},{10,6},{14,10},{7,3},{... | collective-permute-start | bytes 27656 | tf_op jit(solution)/shard_map/ppermute | solution.py:20
  192.5 7.5 %collective-permute-start.34 = (f32[18,18,1]{2,1,0:T(8,128)S(1)}, f32[18,18,1]{2,1,0:T(8,128)S(1)}, u32[]{:S(2)}, u32[]{:S(2)}) collective-permute-start(f32[18,18,1]{2,1,0:T(8,128)S(1)} %get-tuple-element.24), channel_id=1, source_target_pairs={{0,1},{1,2},{2,3},{4,5},{5,6},{6,7},{8,9},{9,10},{10,11},{12,13},{... | collective-permute-start | bytes 3896 | tf_op jit(solution)/shard_map/ppermute | solution.py:18
  197.1 7.3 %collective-permute-start.35 = (f32[18,18,1]{2,1,0:T(8,128)S(1)}, f32[18,18,1]{2,1,0:T(8,128)S(1)}, u32[]{:S(2)}, u32[]{:S(2)}) collective-permute-start(f32[18,18,1]{2,1,0:T(8,128)S(1)} %get-tuple-element.23), channel_id=1, source_target_pairs={{1,0},{2,1},{3,2},{5,4},{6,5},{7,6},{9,8},{10,9},{11,10},{13,12},{... | collective-permute-start | bytes 3896 | tf_op jit(solution)/shard_map/ppermute | solution.py:20
  206.1 2.7 %collective-permute-start.36 = (f32[1,16,128]{2,1,0:T(8,128)S(1)}, f32[1,16,128]{2,1,0:T(8,128)S(1)}, u32[]{:S(2)}, u32[]{:S(2)}) collective-permute-start(f32[1,16,128]{2,1,0:T(8,128)S(1)} %get-tuple-element.55), channel_id=1, source_target_pairs={{0,16},{1,17},{2,18},{3,19},{4,20},{5,21},{6,22},{7,23},{8,24},{9,... | collective-permute-start | bytes 24584 | tf_op jit(solution)/shard_map/ppermute | solution.py:18
  207.5 4.4 %collective-permute-start.37 = (f32[1,16,128]{2,1,0:T(8,128)S(1)}, f32[1,16,128]{2,1,0:T(8,128)S(1)}, u32[]{:S(2)}, u32[]{:S(2)}) collective-permute-start(f32[1,16,128]{2,1,0:T(8,128)S(1)} %get-tuple-element.56), channel_id=1, source_target_pairs={{16,0},{17,1},{18,2},{19,3},{20,4},{21,5},{22,6},{23,7},{24,8},{25... | collective-permute-start | bytes 24584 | tf_op jit(solution)/shard_map/ppermute | solution.py:20
  211.9 3.0 %collective-permute-start.38 = (f32[18,1,128]{2,1,0:T(1,128)S(1)}, f32[18,1,128]{2,1,0:T(1,128)S(1)}, u32[]{:S(2)}, u32[]{:S(2)}) collective-permute-start(f32[18,1,128]{2,1,0:T(1,128)S(1)} %get-tuple-element.37), channel_id=1, source_target_pairs={{0,4},{4,8},{8,12},{1,5},{5,9},{9,13},{2,6},{6,10},{10,14},{3,7},{... | collective-permute-start | bytes 27656 | tf_op jit(solution)/shard_map/ppermute | solution.py:18
  213.6 4.4 %collective-permute-start.39 = (f32[18,1,128]{2,1,0:T(1,128)S(1)}, f32[18,1,128]{2,1,0:T(1,128)S(1)}, u32[]{:S(2)}, u32[]{:S(2)}) collective-permute-start(f32[18,1,128]{2,1,0:T(1,128)S(1)} %get-tuple-element.38), channel_id=1, source_target_pairs={{4,0},{8,4},{12,8},{5,1},{9,5},{13,9},{6,2},{10,6},{14,10},{7,3},{... | collective-permute-start | bytes 27656 | tf_op jit(solution)/shard_map/ppermute | solution.py:20
  218.1 7.5 %collective-permute-start.40 = (f32[18,18,1]{2,1,0:T(8,128)S(1)}, f32[18,18,1]{2,1,0:T(8,128)S(1)}, u32[]{:S(2)}, u32[]{:S(2)}) collective-permute-start(f32[18,18,1]{2,1,0:T(8,128)S(1)} %get-tuple-element.22), channel_id=1, source_target_pairs={{0,1},{1,2},{2,3},{4,5},{5,6},{6,7},{8,9},{9,10},{10,11},{12,13},{... | collective-permute-start | bytes 3896 | tf_op jit(solution)/shard_map/ppermute | solution.py:18
  222.8 7.3 %collective-permute-start.41 = (f32[18,18,1]{2,1,0:T(8,128)S(1)}, f32[18,18,1]{2,1,0:T(8,128)S(1)}, u32[]{:S(2)}, u32[]{:S(2)}) collective-permute-start(f32[18,18,1]{2,1,0:T(8,128)S(1)} %get-tuple-element.21), channel_id=1, source_target_pairs={{1,0},{2,1},{3,2},{5,4},{6,5},{7,6},{9,8},{10,9},{11,10},{13,12},{... | collective-permute-start | bytes 3896 | tf_op jit(solution)/shard_map/ppermute | solution.py:20
  231.8 2.7 %collective-permute-start.42 = (f32[1,16,128]{2,1,0:T(8,128)S(1)}, f32[1,16,128]{2,1,0:T(8,128)S(1)}, u32[]{:S(2)}, u32[]{:S(2)}) collective-permute-start(f32[1,16,128]{2,1,0:T(8,128)S(1)} %get-tuple-element.53), channel_id=1, source_target_pairs={{0,16},{1,17},{2,18},{3,19},{4,20},{5,21},{6,22},{7,23},{8,24},{9,... | collective-permute-start | bytes 24584 | tf_op jit(solution)/shard_map/ppermute | solution.py:18
  233.1 4.4 %collective-permute-start.43 = (f32[1,16,128]{2,1,0:T(8,128)S(1)}, f32[1,16,128]{2,1,0:T(8,128)S(1)}, u32[]{:S(2)}, u32[]{:S(2)}) collective-permute-start(f32[1,16,128]{2,1,0:T(8,128)S(1)} %get-tuple-element.54), channel_id=1, source_target_pairs={{16,0},{17,1},{18,2},{19,3},{20,4},{21,5},{22,6},{23,7},{24,8},{25... | collective-permute-start | bytes 24584 | tf_op jit(solution)/shard_map/ppermute | solution.py:20
  237.5 3.0 %collective-permute-start.44 = (f32[18,1,128]{2,1,0:T(1,128)S(1)}, f32[18,1,128]{2,1,0:T(1,128)S(1)}, u32[]{:S(2)}, u32[]{:S(2)}) collective-permute-start(f32[18,1,128]{2,1,0:T(1,128)S(1)} %get-tuple-element.35), channel_id=1, source_target_pairs={{0,4},{4,8},{8,12},{1,5},{5,9},{9,13},{2,6},{6,10},{10,14},{3,7},{... | collective-permute-start | bytes 27656 | tf_op jit(solution)/shard_map/ppermute | solution.py:18
  239.2 4.4 %collective-permute-start.45 = (f32[18,1,128]{2,1,0:T(1,128)S(1)}, f32[18,1,128]{2,1,0:T(1,128)S(1)}, u32[]{:S(2)}, u32[]{:S(2)}) collective-permute-start(f32[18,1,128]{2,1,0:T(1,128)S(1)} %get-tuple-element.36), channel_id=1, source_target_pairs={{4,0},{8,4},{12,8},{5,1},{9,5},{13,9},{6,2},{10,6},{14,10},{7,3},{... | collective-permute-start | bytes 27656 | tf_op jit(solution)/shard_map/ppermute | solution.py:20
  243.8 7.5 %collective-permute-start.46 = (f32[18,18,1]{2,1,0:T(8,128)S(1)}, f32[18,18,1]{2,1,0:T(8,128)S(1)}, u32[]{:S(2)}, u32[]{:S(2)}) collective-permute-start(f32[18,18,1]{2,1,0:T(8,128)S(1)} %get-tuple-element.20), channel_id=1, source_target_pairs={{0,1},{1,2},{2,3},{4,5},{5,6},{6,7},{8,9},{9,10},{10,11},{12,13},{... | collective-permute-start | bytes 3896 | tf_op jit(solution)/shard_map/ppermute | solution.py:18
  248.4 7.3 %collective-permute-start.47 = (f32[18,18,1]{2,1,0:T(8,128)S(1)}, f32[18,18,1]{2,1,0:T(8,128)S(1)}, u32[]{:S(2)}, u32[]{:S(2)}) collective-permute-start(f32[18,18,1]{2,1,0:T(8,128)S(1)} %get-tuple-element.19), channel_id=1, source_target_pairs={{1,0},{2,1},{3,2},{5,4},{6,5},{7,6},{9,8},{10,9},{11,10},{13,12},{... | collective-permute-start | bytes 3896 | tf_op jit(solution)/shard_map/ppermute | solution.py:20
where the time goes:
time: 259 us; the launch traced here: 258 us
  starting transfers between devices  120 us (46%)
  waiting for transfers between devices  75.2 us (29%)
  blocking collectives  35.2 us (14%)
  local copies, waits for them, and re-layouts  13.7 us (5%)
  other arithmetic  8.13 us (3%)
  between operations  5.66 us (2%)
    ppermute x24, starting transfers between devices, padded(): lax.ppermute(tail, axis, [(i, (i + 1) % count) for i in range(ends)])  83.6 us
    ppermute x24, waiting for transfers between devices, padded(): lax.ppermute(head, axis, [((i + 1) % count, i) for i in range(ends)])  69.7 us
    ppermute x24, starting transfers between devices, padded(): lax.ppermute(head, axis, [((i + 1) % count, i) for i in range(ends)])  36.5 us
    psum x1, blocking collectives, on_device(): lax.psum((jnp.sum(vector * vector), jnp.sum(previous * previous)), ('gx',...  35.2 us
    dynamic_update_slice x8, local copies, waits for them, and re-layouts, stitch(): lax.dynamic_update_slice_in_dim(buffer, after, planes_here + margin, axis...  11.4 us
    ppermute x24, waiting for transfers between devices, padded(): lax.ppermute(tail, axis, [(i, (i + 1) % count) for i in range(ends)])  5.49 us
  transfers between devices with their start and end apart: 48, of which 26 were waited for; matrix products, arithmetic and copies ran while one was open for 1% of the time, Pallas kernels for 0%

commit v1 on v0

v1 whole, which is shorter than its diff:
```python
import functools

import numpy as np
import jax
import jax.numpy as jnp
from jax import lax
from jax.experimental import pallas as pl
from jax.experimental.pallas import tpu as pltpu
from jax.sharding import PartitionSpec as P

POWER = 3
DEGREE = 4
AXES = ("gx", "gy", "gz")
SUM_ORDER = ("gz", "gx", "gy")
MESH = pl.DeviceIdType.MESH


def chebyshev_polynomials():
    basis = np.zeros(DEGREE + 2)
    basis[0] = 1.0
    times = lambda poly: np.concatenate([[0.0], poly[:-1]])
    sharpness = 1.2
    ratio = 1.0 / sharpness
    answer = np.zeros_like(basis)
    residue = basis.copy()
    direction = basis / 0.6
    for section in range(DEGREE):
        answer = answer + direction
        residue = residue - times(direction)
        if section < DEGREE - 1:
            fresh = 1.0 / (2.0 * sharpness - ratio)
            direction = fresh * ratio * direction + 2.0 * fresh / 0.5 * residue
            ratio = fresh
    return [float(v) for v in answer[:DEGREE]], [float(v) for v in residue[: DEGREE + 1]]


def kernel(
    sizes, counts_ref, rhs_ref, coef_ref, start_ref, sol_ref, res_ref,
    pow_ref, kry_ref, wx_ref, wym_ref, wyp_ref, wzm_ref, wzp_ref, diag_ref,
    sx, sy, sz, rx, ry, rz, sums_gz, sums_gx, sums_gy, send_sem, recv_sem, sum_send, sum_recv,
):
    X, Y, S = rhs_ref.shape
    me = {a: lax.axis_index(a) for a in AXES}
    has = {}
    for a in AXES:
        has[a] = (me[a] > 0, me[a] < sizes[a] - 1)

    barrier = pltpu.get_barrier_semaphore()
    for a in AXES:
        for step in range(1, sizes[a]):
            pl.semaphore_signal(
                barrier, inc=1, device_id={a: lax.rem(me[a] + step, sizes[a])}, device_id_type=MESH
            )

    lane = lax.broadcasted_iota(jnp.int32, (Y, S), 1)
    row = lax.broadcasted_iota(jnp.int32, (Y, S), 0)
    planes = counts_ref[me["gz"]]
    alive = lane < planes
    is_first = lane == 0
    is_last = lane == planes - 1
    top = row == 0
    bottom = row == Y - 1

    def descriptor(msg, fields, axis, side):
        send, recv, which = {"gx": (sx, rx, 0), "gy": (sy, ry, 1), "gz": (sz, rz, 2)}[axis]
        if axis == "gz":
            src, dst = send.at[msg, side], recv.at[msg, 1 - side]
        else:
            src = send.at[msg, side, pl.ds(0, fields)]
            dst = recv.at[msg, 1 - side, pl.ds(0, fields)]
        return pltpu.make_async_remote_copy(
            src_ref=src,
            dst_ref=dst,
            send_sem=send_sem.at[msg, which, side],
            recv_sem=recv_sem.at[msg, which, 1 - side],
            device_id={axis: me[axis] + (1 if side else -1)},
            device_id_type=MESH,
        )

    class Packer:
        def __init__(self, msg):
            self.msg = msg
            self.low = jnp.zeros((Y, S), jnp.float32)
            self.high = jnp.zeros((Y, S), jnp.float32)

        def put(self, f, x, value):
            m = self.msg
            if x == 0:
                sx[m, 0, f] = value
            if x == X - 1:
                sx[m, 1, f] = value
            sy[m, 0, f, x : x + 1, :] = value[0:1, :]
            sy[m, 1, f, x : x + 1, :] = value[Y - 1 : Y, :]
            here = lane == f * X + x
            self.low = jnp.where(here, value[:, 0:1], self.low)
            tail = jnp.sum(jnp.where(is_last, value, 0.0), axis=1, keepdims=True)
            self.high = jnp.where(here, tail, self.high)

        def finish(self):
            sz[self.msg, 0] = self.low
            sz[self.msg, 1] = self.high

    def launch(msg, fields):
        for axis in AXES:
            for side in (0, 1):
                @pl.when(has[axis][side])
                def _(axis=axis, side=side):
                    descriptor(msg, fields, axis, side).start()

    def receive(msg, fields):
        for axis in AXES:
            for side in (0, 1):
                @pl.when(has[axis][1 - side])
                def _(axis=axis, side=side):
                    descriptor(msg, fields, axis, side).wait_recv()

    def drain(msg, fields):
        for axis in AXES:
            for side in (0, 1):
                @pl.when(has[axis][side])
                def _(axis=axis, side=side):
                    descriptor(msg, fields, axis, side).wait_send()

    def blank():
        for axis, recv in (("gx", rx), ("gy", ry), ("gz", rz)):
            for side in (0, 1):
                @pl.when(jnp.logical_not(has[axis][side]))
                def _(recv=recv, side=side):
                    for msg in range(recv.shape[0]):
                        recv[msg, side] = jnp.zeros(recv.shape[2:], jnp.float32)

    def around(load, msg, f, x, zlow, zhigh):
        centre = load(x)
        below = rx[msg, 0, f] if x == 0 else load(x - 1)
        above = rx[msg, 1, f] if x == X - 1 else load(x + 1)
        ym = jnp.where(top, ry[msg, 0, f, x : x + 1, :], pltpu.roll(centre, 1, 0))
        yp = jnp.where(bottom, ry[msg, 1, f, x : x + 1, :], pltpu.roll(centre, Y - 1, 0))
        at = f * X + x
        zm = jnp.where(is_first, zlow[:, at : at + 1], pltpu.roll(centre, 1, 1))
        zp = jnp.where(is_last, zhigh[:, at : at + 1], pltpu.roll(centre, S - 1, 1))
        return centre, below, above, ym, yp, zm, zp

    def face(centre, other):
        other = jnp.where(other > 0, other, centre)
        return jnp.where(alive, 0.5 * (centre + other), 0.0)

    def weights(msg):
        zlow, zhigh = rz[msg, 0], rz[msg, 1]
        under = None
        for x in range(X):
            c, below, above, ym, yp, zm, zp = around(lambda i: coef_ref[i], msg, 0, x, zlow, zhigh)
            if x == 0:
                under = face(c, below)
                wx_ref[0] = under
            over = face(c, above)
            parts = [face(c, o) for o in (ym, yp, zm, zp)]
            wx_ref[x + 1] = over
            wym_ref[x], wyp_ref[x], wzm_ref[x], wzp_ref[x] = parts
            diag_ref[x] = (under + over) + (parts[0] + parts[1]) + (parts[2] + parts[3])
            under = over

    def operate(load, msg, f, emit):
        zlow, zhigh = rz[msg, 0], rz[msg, 1]
        for x in range(X):
            c, below, above, ym, yp, zm, zp = around(load, msg, f, x, zlow, zhigh)
            near = wx_ref[x] * below + wx_ref[x + 1] * above
            near = near + (wym_ref[x] * ym + wyp_ref[x] * yp)
            near = near + (wzm_ref[x] * zm + wzp_ref[x] * zp)
            emit(x, diag_ref[x] * c - near)

    def step(load, msg, f, store, out_msg, total=None):
        pack = Packer(out_msg) if out_msg is not None else None
        box = [total]

        def emit(x, value):
            if store is not None:
                store[x] = value
            if pack is not None:
                pack.put(0, x, value)
            if total is not None:
                box[0] = box[0] + value * value

        operate(load, msg, f, emit)
        if pack is not None:
            pack.finish()
            launch(out_msg, 1)
        return box[0]

    pack = Packer(0)
    for x in range(X):
        pack.put(0, x, coef_ref[x])
        pack.put(1, x, start_ref[x])
    pack.finish()
    pack = Packer(1)
    for x in range(X):
        pack.put(0, x, rhs_ref[x])
    pack.finish()
    blank()
    pl.semaphore_wait(barrier, sum(sizes[a] - 1 for a in AXES))
    launch(0, 2)
    launch(1, 1)

    zero = jnp.zeros((Y, S), jnp.float32)
    receive(0, 2)
    weights(0)
    step(lambda x: start_ref[x], 0, 1, pow_ref.at[0], 2)
    receive(1, 1)
    step(lambda x: rhs_ref[x], 1, 0, kry_ref.at[0], 4)
    receive(2, 1)
    lower = step(lambda x: pow_ref[0, x], 2, 0, pow_ref.at[1], 3, zero)
    receive(4, 1)
    step(lambda x: kry_ref[0, x], 4, 0, kry_ref.at[1], 5)
    receive(3, 1)
    upper = step(lambda x: pow_ref[1, x], 3, 0, None, None, zero)

    sums = {"gz": sums_gz, "gx": sums_gx, "gy": sums_gy}
    pick = lax.broadcasted_iota(jnp.int32, (8, S), 0) < 4
    mine = jnp.where(pick, jnp.sum(upper, keepdims=True), jnp.sum(lower, keepdims=True))

    def sum_copy(k, axis, peer):
        buf = sums[axis]
        return pltpu.make_async_remote_copy(
            src_ref=buf.at[me[axis]],
            dst_ref=buf.at[me[axis]],
            send_sem=sum_send.at[k, peer],
            recv_sem=sum_recv.at[k, me[axis]],
            device_id={axis: peer},
            device_id_type=MESH,
        )

    def sum_arrival(k, axis, peer):
        buf = sums[axis]
        return pltpu.make_async_remote_copy(
            src_ref=buf.at[peer],
            dst_ref=buf.at[peer],
            send_sem=sum_send.at[k, peer],
            recv_sem=sum_recv.at[k, peer],
            device_id={axis: peer},
            device_id_type=MESH,
        )

    def sums_out(k, value):
        axis = SUM_ORDER[k]
        sums[axis][me[axis]] = value
        for hop in range(1, sizes[axis]):
            sum_copy(k, axis, lax.rem(me[axis] + hop, sizes[axis])).start()

    def sums_in(k):
        axis = SUM_ORDER[k]
        for hop in range(1, sizes[axis]):
            sum_arrival(k, axis, lax.rem(me[axis] + hop, sizes[axis])).wait_recv()
        value = sums[axis][0]
        for i in range(1, sizes[axis]):
            value = value + sums[axis][i]
        return value

    sums_out(0, mine)
    receive(5, 1)
    step(lambda x: kry_ref[1, x], 5, 0, kry_ref.at[2], 6)
    sums_out(1, sums_in(0))
    receive(6, 1)
    step(lambda x: kry_ref[2, x], 6, 0, kry_ref.at[3], None)
    sums_out(2, sums_in(1))
    total = sums_in(2)
    inverse = jnp.sqrt(total[4:5, :] / total[0:1, :])
    answer, residue = chebyshev_polynomials()
    power = [jnp.ones_like(inverse)]
    for _ in range(DEGREE):
        power.append(power[-1] * inverse)
    for x in range(X):
        krylov = [jnp.where(alive, rhs_ref[x], 0.0)] + [kry_ref[i, x] for i in range(DEGREE)]
        sol = krylov[0] * (answer[0] * power[1])
        res = krylov[0] * residue[0]
        for i in range(1, DEGREE):
            sol = sol + krylov[i] * (answer[i] * power[i + 1])
        for i in range(1, DEGREE + 1):
            res = res + krylov[i] * (residue[i] * power[i])
        sol_ref[x] = sol
        res_ref[x] = res

    drain(0, 2)
    for msg in range(1, 7):
        drain(msg, 1)
    for k, axis in enumerate(SUM_ORDER):
        for hop in range(1, sizes[axis]):
            sum_copy(k, axis, lax.rem(me[axis] + hop, sizes[axis])).wait_send()


def on_device(sizes, right_side, coefficient, start_vector, plane_counts):
    X, Y, S = right_side.shape
    f32 = jnp.float32
    most = max(sizes.values())
    vmem = pl.BlockSpec(memory_space=pltpu.VMEM)
    return pl.pallas_call(
        functools.partial(kernel, sizes),
        out_shape=(jax.ShapeDtypeStruct((X, Y, S), f32),) * 2,
        in_specs=[pl.BlockSpec(memory_space=pltpu.SMEM), vmem, vmem, vmem],
        out_specs=(vmem, vmem),
        scratch_shapes=[
            pltpu.VMEM((POWER - 1, X, Y, S), f32),
            pltpu.VMEM((DEGREE, X, Y, S), f32),
            pltpu.VMEM((X + 1, Y, S), f32),
            *[pltpu.VMEM((X, Y, S), f32)] * 5,
            pltpu.VMEM((7, 2, 2, Y, S), f32),
            pltpu.VMEM((7, 2, 2, X, S), f32),
            pltpu.VMEM((7, 2, Y, S), f32),
            pltpu.VMEM((7, 2, 2, Y, S), f32),
            pltpu.VMEM((7, 2, 2, X, S), f32),
            pltpu.VMEM((7, 2, Y, S), f32),
            pltpu.VMEM((sizes["gz"], 8, S), f32),
            pltpu.VMEM((sizes["gx"], 8, S), f32),
            pltpu.VMEM((sizes["gy"], 8, S), f32),
            pltpu.SemaphoreType.DMA((7, 3, 2)),
            pltpu.SemaphoreType.DMA((7, 3, 2)),
            pltpu.SemaphoreType.DMA((3, most)),
            pltpu.SemaphoreType.DMA((3, most)),
        ],
        compiler_params=pltpu.CompilerParams(collective_id=0, has_side_effects=True),
    )(plane_counts, right_side, coefficient, start_vector)


def solution(mesh):
    sizes = {a: mesh.shape[a] for a in AXES}
    spec = P("gx", "gy", "gz")
    return jax.shard_map(
        functools.partial(on_device, sizes),
        mesh=mesh,
        in_specs=(spec, spec, spec, P()),
        out_specs=(spec, spec),
        check_vma=False,
    )
```

time: 259 us -> 31.8 us (0.12)
  the two profiles are of different devices: /device:TPU:1 before, /device:TPU:0 now
where the time goes in v1:
time: 31.8 us; the launch traced here: 31.7 us
  Pallas kernels  28.7 us (90%)
  local copies, waits for them, and re-layouts  2.26 us (7%)
  between operations  0.65 us (2%)
    pallas_call x1, Pallas kernels, on_device(): pl.pallas_call(functools.partial(kernel, sizes), out_shape=(jax.ShapeDtyp...  28.7 us
    unnamed x4, local copies, waits for them, and re-layouts  2.26 us

profile of v1, /device:TPU:0, one launch (start us, length us, event | category | flops | bytes accessed | tf_op | source)
XLA Modules:
  0.0 31.7 jit_solution(1432386471496397557)
XLA Ops:
  0.6 28.7 %shard_map.59 = (f32[16,16,128]{2,1,0:T(8,128)}, f32[16,16,128]{2,1,0:T(8,128)}) custom-call(s32[4]{0:T(128)} %counts_ref.1, f32[16,16,128]{2,1,0:T(8,128)} %rhs_ref.1, f32[16,16,128]{2,1,0:T(8,128)} %coef_ref.1, f32[16,16,128]{2,1,0:T(8,128)} %start_ref.1), custom_call_target="tpu_custom_call" | custom-call | tf_op jit(solution)/shard_map/pallas_call | solution.py:294
  29.4 0.0 copy-start
  29.4 1.6 %copy.8 = f32[16,16,128]{2,1,0:T(8,128)} copy(f32[16,16,128]{2,1,0:T(8,128)} %get-tuple-element.4) | data formatting | bytes 262144
  31.0 0.0 copy-done
  31.0 0.7 %copy.9 = f32[16,16,128]{2,1,0:T(8,128)} copy(f32[16,16,128]{2,1,0:T(8,128)S(1)} %copy-done) | data formatting | bytes 262144
Async XLA Ops:
  29.4 1.6 %copy-start = (f32[16,16,128]{2,1,0:T(8,128)S(1)}, f32[16,16,128]{2,1,0:T(8,128)}, u32[]{:S(2)}) copy-start(f32[16,16,128]{2,1,0:T(8,128)} %get-tuple-element.5) | copy-start | bytes 393220

commit v2 on v1

v2 whole, which is shorter than its diff:
```python
import functools

import numpy as np
import jax
import jax.numpy as jnp
from jax import lax
from jax.experimental import pallas as pl
from jax.experimental.pallas import tpu as pltpu
from jax.sharding import PartitionSpec as P

POWER = 3
DEGREE = 4
AXES = ("gx", "gy", "gz")
DIRECT_LIMIT = 64
START, RIGHT, V1, V2, K1, K2, K3 = range(7)
ENTRIES = {START: (0, 2, 0), RIGHT: (2, 1, 2), V1: (3, 1, 1), V2: (4, 1, 0), K1: (5, 1, 3), K2: (6, 1, 2), K3: (7, 1, 3)}
MESH = pl.DeviceIdType.MESH


def chebyshev_polynomials():
    basis = np.zeros(DEGREE + 2)
    basis[0] = 1.0
    times = lambda poly: np.concatenate([[0.0], poly[:-1]])
    sharpness = 1.2
    ratio = 1.0 / sharpness
    answer = np.zeros_like(basis)
    residue = basis.copy()
    direction = basis / 0.6
    for section in range(DEGREE):
        answer = answer + direction
        residue = residue - times(direction)
        if section < DEGREE - 1:
            fresh = 1.0 / (2.0 * sharpness - ratio)
            direction = fresh * ratio * direction + 2.0 * fresh / 0.5 * residue
            ratio = fresh
    return [float(v) for v in answer[:DEGREE]], [float(v) for v in residue[: DEGREE + 1]]


def plan(sizes):
    if sizes["gx"] * sizes["gy"] * sizes["gz"] <= DIRECT_LIMIT:
        return (("gx", "gy", "gz"),), sum(sizes.values()) - len(sizes) - 1
    return (("gz",), ("gx",), ("gy",)), 0


def offsets(sizes, axes):
    grid = list(np.ndindex(*[sizes[a] for a in axes]))
    return [dict(zip(axes, map(int, o))) for o in grid if any(o)]


def kernel(
    sizes, counts_ref, rhs_ref, coef_ref, start_ref, kry_out, total_ref,
    pow_ref, kry_ref, wx_ref, wym_ref, wyp_ref, wzm_ref, wzp_ref, diag_ref,
    sx, sy, sz, rx, ry, rz, own_ref, sums_ref, send_sem, recv_sem, sum_send, sum_recv, out_sem, flood_sem,
):
    X, Y, S = rhs_ref.shape
    me = {a: lax.axis_index(a) for a in AXES}
    stages, floods = plan(sizes)
    has = {}
    for a in AXES:
        has[a] = (me[a] > 0, me[a] < sizes[a] - 1)
    neighbours = sum(h.astype(jnp.int32) for a in AXES for h in has[a])

    def greet(sem):
        for a in AXES:
            for side in (0, 1):
                @pl.when(has[a][side])
                def _(a=a, side=side):
                    pl.semaphore_signal(
                        sem, inc=1, device_id={a: me[a] + (1 if side else -1)}, device_id_type=MESH
                    )

    flooded = [0]

    def flood(rounds):
        for _ in range(rounds):
            if flooded[0] < floods:
                greet(flood_sem.at[flooded[0]])
                pl.semaphore_wait(flood_sem.at[flooded[0]], neighbours)
                flooded[0] += 1

    barrier = pltpu.get_barrier_semaphore()
    if floods:
        greet(barrier)
        arrivals = neighbours
    else:
        for a in AXES:
            for step in range(1, sizes[a]):
                pl.semaphore_signal(
                    barrier, inc=1, device_id={a: lax.rem(me[a] + step, sizes[a])}, device_id_type=MESH
                )
        arrivals = sum(sizes[a] - 1 for a in AXES)

    lane = lax.broadcasted_iota(jnp.int32, (Y, S), 1)
    row = lax.broadcasted_iota(jnp.int32, (Y, S), 0)
    planes = counts_ref[me["gz"]]
    alive = lane < planes
    is_first = lane == 0
    is_last = lane == planes - 1
    top = row == 0
    bottom = row == Y - 1

    def descriptor(msg, axis, side):
        send, recv, which = {"gx": (sx, rx, 0), "gy": (sy, ry, 1), "gz": (sz, rz, 2)}[axis]
        entry, fields, arrival = ENTRIES[msg]
        at = msg if axis == "gz" else pl.ds(entry, fields)
        return pltpu.make_async_remote_copy(
            src_ref=send.at[side, at],
            dst_ref=recv.at[1 - side, at],
            send_sem=send_sem.at[which, side],
            recv_sem=recv_sem.at[arrival, which, 1 - side],
            device_id={axis: me[axis] + (1 if side else -1)},
            device_id_type=MESH,
        )

    class Packer:
        def __init__(self, msg):
            self.msg = msg
            self.low = jnp.zeros((Y, S), jnp.float32)
            self.high = jnp.zeros((Y, S), jnp.float32)

        def put(self, f, x, value):
            e = ENTRIES[self.msg][0] + f
            if x == 0:
                sx[0, e] = value
            if x == X - 1:
                sx[1, e] = value
            sy[0, e, x : x + 1, :] = value[0:1, :]
            sy[1, e, x : x + 1, :] = value[Y - 1 : Y, :]
            here = lane == f * X + x
            self.low = jnp.where(here, value[:, 0:1], self.low)
            tail = jnp.sum(jnp.where(is_last, value, 0.0), axis=1, keepdims=True)
            self.high = jnp.where(here, tail, self.high)

        def finish(self):
            sz[0, self.msg] = self.low
            sz[1, self.msg] = self.high

    def launch(msg):
        for axis in AXES:
            for side in (0, 1):
                @pl.when(has[axis][side])
                def _(axis=axis, side=side):
                    descriptor(msg, axis, side).start()

    def receive(msg):
        for axis in AXES:
            for side in (0, 1):
                @pl.when(has[axis][1 - side])
                def _(axis=axis, side=side):
                    descriptor(msg, axis, side).wait_recv()

    def drain():
        for which, (axis, send, recv) in enumerate((("gx", sx, rx), ("gy", sy, ry), ("gz", sz, rz))):
            for side in (0, 1):
                @pl.when(has[axis][side])
                def _(axis=axis, side=side, which=which, send=send, recv=recv):
                    pltpu.make_async_remote_copy(
                        src_ref=send.at[side],
                        dst_ref=recv.at[1 - side],
                        send_sem=send_sem.at[which, side],
                        recv_sem=recv_sem.at[0, which, 1 - side],
                        device_id={axis: me[axis] + (1 if side else -1)},
                        device_id_type=MESH,
                    ).wait_send()

    def blank():
        for axis, recv in (("gx", rx), ("gy", ry), ("gz", rz)):
            for side in (0, 1):
                @pl.when(jnp.logical_not(has[axis][side]))
                def _(recv=recv, side=side):
                    recv[side] = jnp.zeros(recv.shape[1:], jnp.float32)

    def around(load, msg, f, x, zlow, zhigh):
        centre = load(x)
        below = rx[0, ENTRIES[msg][0] + f] if x == 0 else load(x - 1)
        above = rx[1, ENTRIES[msg][0] + f] if x == X - 1 else load(x + 1)
        ym = jnp.where(top, ry[0, ENTRIES[msg][0] + f, x : x + 1, :], pltpu.roll(centre, 1, 0))
        yp = jnp.where(bottom, ry[1, ENTRIES[msg][0] + f, x : x + 1, :], pltpu.roll(centre, Y - 1, 0))
        at = f * X + x
        zm = jnp.where(is_first, zlow[:, at : at + 1], pltpu.roll(centre, 1, 1))
        zp = jnp.where(is_last, zhigh[:, at : at + 1], pltpu.roll(centre, S - 1, 1))
        return centre, below, above, ym, yp, zm, zp

    def face(centre, other):
        other = jnp.where(other > 0, other, centre)
        return jnp.where(alive, 0.5 * (centre + other), 0.0)

    def weights(msg):
        zlow, zhigh = rz[0, msg], rz[1, msg]
        under = None
        for x in range(X):
            c, below, above, ym, yp, zm, zp = around(lambda i: coef_ref[i], msg, 0, x, zlow, zhigh)
            if x == 0:
                under = face(c, below)
                wx_ref[0] = under
            over = face(c, above)
            parts = [face(c, o) for o in (ym, yp, zm, zp)]
            wx_ref[x + 1] = over
            wym_ref[x], wyp_ref[x], wzm_ref[x], wzp_ref[x] = parts
            diag_ref[x] = (under + over) + (parts[0] + parts[1]) + (parts[2] + parts[3])
            under = over

    def operate(load, msg, f, emit):
        zlow, zhigh = rz[0, msg], rz[1, msg]
        for x in range(X):
            c, below, above, ym, yp, zm, zp = around(load, msg, f, x, zlow, zhigh)
            near = wx_ref[x] * below + wx_ref[x + 1] * above
            near = near + (wym_ref[x] * ym + wyp_ref[x] * yp)
            near = near + (wzm_ref[x] * zm + wzp_ref[x] * zp)
            emit(x, diag_ref[x] * c - near)

    def step(load, msg, f, store, out_msg, total=None):
        pack = Packer(out_msg) if out_msg is not None else None
        box = [total]

        def emit(x, value):
            if store is not None:
                store[x] = value
            if pack is not None:
                pack.put(0, x, value)
            if total is not None:
                box[0] = box[0] + value * value

        operate(load, msg, f, emit)
        if pack is not None:
            pack.finish()
            launch(out_msg)
        return box[0]

    pack = Packer(START)
    for x in range(X):
        pack.put(0, x, coef_ref[x])
        pack.put(1, x, start_ref[x])
    pack.finish()
    pack = Packer(RIGHT)
    for x in range(X):
        pack.put(0, x, rhs_ref[x])
    pack.finish()
    blank()
    pl.semaphore_wait(barrier, arrivals)
    launch(START)
    launch(RIGHT)

    def out_copy(i):
        return pltpu.make_async_copy(kry_ref.at[i], kry_out.at[i], out_sem.at[i])

    def krylov(i):
        source, msg, out_msg = ((None, RIGHT, K1), (0, K1, K2), (1, K2, K3), (2, K3, None))[i]
        load = (lambda x: rhs_ref[x]) if source is None else (lambda x: kry_ref[source, x])
        receive(msg)
        step(load, msg, 0, kry_ref.at[i], out_msg)
        out_copy(i).start()

    zero = jnp.zeros((Y, S), jnp.float32)
    flood(2)
    receive(START)
    weights(START)
    step(lambda x: start_ref[x], START, 1, pow_ref.at[0], V1)
    krylov(0)
    flood(2)
    receive(V1)
    lower = step(lambda x: pow_ref[0, x], V1, 0, pow_ref.at[1], V2, zero)
    krylov(1)
    flood(floods)
    receive(V2)
    upper = step(lambda x: pow_ref[1, x], V2, 0, None, None, zero)

    pick = lax.broadcasted_iota(jnp.int32, (8, S), 1) < S // 2
    total = jnp.where(pick, jnp.sum(upper, keepdims=True), jnp.sum(lower, keepdims=True))

    def sum_copy(k, slot, offset):
        return pltpu.make_async_remote_copy(
            src_ref=own_ref.at[k, pl.ds(0, 1)],
            dst_ref=sums_ref.at[k, pl.ds(slot, 1)],
            send_sem=sum_send.at[k],
            recv_sem=sum_recv.at[k],
            device_id={a: lax.rem(me[a] + d, sizes[a]) for a, d in offset.items()},
            device_id_type=MESH,
        )

    def all_sums(k, count):
        whole = sums_ref.at[k, pl.ds(0, count)]
        return pltpu.make_async_remote_copy(
            src_ref=whole,
            dst_ref=whole,
            send_sem=sum_send.at[k],
            recv_sem=sum_recv.at[k],
            device_id={"gz": lax.rem(me["gz"] + 1, sizes["gz"])},
            device_id_type=MESH,
        )

    for k, axes in enumerate(stages):
        own_ref[k] = total
        others = offsets(sizes, axes)
        for slot, offset in enumerate(others):
            sum_copy(k, slot, offset).start()
        if k == 0:
            krylov(2)
        if k == len(stages) - 1:
            krylov(3)
        all_sums(k, len(others)).wait_recv()
        total = total + jnp.sum(sums_ref[k, 0 : len(others), :], axis=0, keepdims=True)
    total_ref[...] = total
    for i in range(DEGREE):
        out_copy(i).wait()
    drain()
    for k, axes in enumerate(stages):
        all_sums(k, len(offsets(sizes, axes))).wait_send()


def combine(counts_ref, total_ref, rhs_ref, kry_ref, sol_ref, res_ref):
    X, Y, S = rhs_ref.shape
    alive = lax.broadcasted_iota(jnp.int32, (Y, S), 1) < counts_ref[lax.axis_index("gz")]
    inverse = jnp.sqrt(total_ref[0:1, S - 1 : S] / total_ref[0:1, 0:1])
    power = [jnp.ones_like(inverse)]
    for _ in range(DEGREE):
        power.append(power[-1] * inverse)
    answer, residue = chebyshev_polynomials()
    scale_sol = [jnp.broadcast_to(answer[i] * power[i + 1], (Y, S)) for i in range(DEGREE)]
    scale_res = [jnp.broadcast_to(residue[i] * power[i], (Y, S)) for i in range(DEGREE + 1)]
    for x in range(X):
        terms = [jnp.where(alive, rhs_ref[x], 0.0)] + [kry_ref[i, x] for i in range(DEGREE)]
        sol_ref[x] = sum(terms[i] * scale_sol[i] for i in range(DEGREE))
        res_ref[x] = sum(terms[i] * scale_res[i] for i in range(DEGREE + 1))


def on_device(sizes, right_side, coefficient, start_vector, plane_counts):
    X, Y, S = right_side.shape
    f32 = jnp.float32
    stages, floods = plan(sizes)
    most = max(len(offsets(sizes, axes)) for axes in stages)
    vmem = pl.BlockSpec(memory_space=pltpu.VMEM)
    krylov, total = pl.pallas_call(
        functools.partial(kernel, sizes),
        out_shape=(jax.ShapeDtypeStruct((DEGREE, X, Y, S), f32), jax.ShapeDtypeStruct((8, S), f32)),
        in_specs=[pl.BlockSpec(memory_space=pltpu.SMEM), vmem, vmem, vmem],
        out_specs=(pl.BlockSpec(memory_space=pl.ANY), vmem),
        scratch_shapes=[
            pltpu.VMEM((POWER - 1, X, Y, S), f32),
            pltpu.VMEM((DEGREE, X, Y, S), f32),
            pltpu.VMEM((X + 1, Y, S), f32),
            *[pltpu.VMEM((X, Y, S), f32)] * 5,
            *[pltpu.VMEM((2, 8, Y, S), f32), pltpu.VMEM((2, 8, X, S), f32), pltpu.VMEM((2, 7, Y, S), f32)] * 2,
            pltpu.VMEM((len(stages), 8, S), f32),
            pltpu.VMEM((len(stages), -(-most // 8) * 8, S), f32),
            pltpu.SemaphoreType.DMA((3, 2)),
            pltpu.SemaphoreType.DMA((4, 3, 2)),
            pltpu.SemaphoreType.DMA((len(stages),)),
            pltpu.SemaphoreType.DMA((len(stages),)),
            pltpu.SemaphoreType.DMA((DEGREE,)),
            pltpu.SemaphoreType.REGULAR((max(floods, 1),)),
        ],
        compiler_params=pltpu.CompilerParams(collective_id=0, has_side_effects=True),
    )(plane_counts, right_side, coefficient, start_vector)
    return pl.pallas_call(
        combine,
        out_shape=(jax.ShapeDtypeStruct((X, Y, S), f32),) * 2,
        in_specs=[pl.BlockSpec(memory_space=pltpu.SMEM), vmem, vmem, vmem],
        out_specs=(vmem, vmem),
    )(plane_counts, total, right_side, krylov)


def solution(mesh):
    sizes = {a: mesh.shape[a] for a in AXES}
    spec = P("gx", "gy", "gz")
    return jax.shard_map(
        functools.partial(on_device, sizes),
        mesh=mesh,
        in_specs=(spec, spec, spec, P()),
        out_specs=(spec, spec),
        check_vma=False,
    )
```

time: 31.8 us -> 27.1 us (0.85)
  the two profiles are of different devices: /device:TPU:0 before, /device:TPU:1 now
where the time goes in v2:
time: 27.1 us; the launch traced here: 27 us
  Pallas kernels  26.3 us (97%)
  between operations  0.64 us (2%)
    pallas_call x1, Pallas kernels, on_device(): pl.pallas_call(functools.partial(kernel, sizes), out_shape=(jax.ShapeDtyp...  24.3 us
    pallas_call x1, Pallas kernels, on_device(): pl.pallas_call(combine, out_shape=(jax.ShapeDtypeStruct((X, Y, S), f32),)...  2.05 us

profile of v2, /device:TPU:1, one launch (start us, length us, event | category | flops | bytes accessed | tf_op | source)
XLA Modules:
  0.0 27.0 jit_solution(6347271945920400472)
XLA Ops:
  0.6 24.3 %shard_map.59 = (f32[4,16,16,128]{3,2,1,0:T(8,128)}, f32[8,128]{1,0:T(8,128)}) custom-call(s32[4]{0:T(128)} %counts_ref.3, f32[16,16,128]{2,1,0:T(8,128)} %rhs_ref.3, f32[16,16,128]{2,1,0:T(8,128)} %coef_ref.1, f32[16,16,128]{2,1,0:T(8,128)} %start_ref.1), custom_call_target="tpu_custom_call" | custom-call | tf_op jit(solution)/shard_map/pallas_call | solution.py:333
  24.9 2.1 %shard_map.60 = (f32[16,16,128]{2,1,0:T(8,128)}, f32[16,16,128]{2,1,0:T(8,128)}) custom-call(s32[4]{0:T(128)} %counts_ref.3, f32[8,128]{1,0:T(8,128)} %get-tuple-element.4.total_ref, f32[16,16,128]{2,1,0:T(8,128)} %rhs_ref.3, f32[4,16,16,128]{3,2,1,0:T(8,128)} %get-tuple-element.5.kry_ref), custom_call_target="tpu_custom_call" | custom-call | tf_op jit(solution)/shard_map/pallas_call | solution.py:355

commit v3 on v2

--- a/solution.py
+++ b/solution.py
@@ -38,7 +38,7 @@
 
 def plan(sizes):
     if sizes["gx"] * sizes["gy"] * sizes["gz"] <= DIRECT_LIMIT:
-        return (("gx", "gy", "gz"),), sum(sizes.values()) - len(sizes) - 1
+        return (("gx", "gy", "gz"),), max(sum(sizes.values()) - len(sizes) - 2, 1)
     return (("gz",), ("gx",), ("gy",)), 0
 
 
@@ -48,13 +48,19 @@
 
 
 def kernel(
-    sizes, counts_ref, rhs_ref, coef_ref, start_ref, kry_out, total_ref,
+    sizes, counts_ref, rhs_hbm, coef_hbm, start_hbm, kry_out, total_ref, rhs_ref, coef_ref, start_ref,
     pow_ref, kry_ref, wx_ref, wym_ref, wyp_ref, wzm_ref, wzp_ref, diag_ref,
-    sx, sy, sz, rx, ry, rz, own_ref, sums_ref, send_sem, recv_sem, sum_send, sum_recv, out_sem, flood_sem,
+    sx, sy, sz, rx, ry, rz, own_ref, sums_ref, send_sem, recv_sem, sum_send, sum_recv, out_sem, flood_sem, in_sem,
 ):
     X, Y, S = rhs_ref.shape
     me = {a: lax.axis_index(a) for a in AXES}
     stages, floods = plan(sizes)
+    loads = [
+        pltpu.make_async_copy(src, dst, in_sem.at[i])
+        for i, (src, dst) in enumerate(((coef_hbm, coef_ref), (start_hbm, start_ref), (rhs_hbm, rhs_ref)))
+    ]
+    for load in loads:
+        load.start()
     has = {}
     for a in AXES:
         has[a] = (me[a] > 0, me[a] < sizes[a] - 1)
@@ -227,18 +233,21 @@
             launch(out_msg)
         return box[0]
 
+    blank()
+    loads[0].wait()
+    loads[1].wait()
     pack = Packer(START)
     for x in range(X):
         pack.put(0, x, coef_ref[x])
         pack.put(1, x, start_ref[x])
     pack.finish()
+    pl.semaphore_wait(barrier, arrivals)
+    launch(START)
+    loads[2].wait()
     pack = Packer(RIGHT)
     for x in range(X):
         pack.put(0, x, rhs_ref[x])
     pack.finish()
-    blank()
-    pl.semaphore_wait(barrier, arrivals)
-    launch(START)
     launch(RIGHT)
 
     def out_copy(i):
@@ -252,12 +261,11 @@
         out_copy(i).start()
 
     zero = jnp.zeros((Y, S), jnp.float32)
-    flood(2)
+    flood(3)
     receive(START)
     weights(START)
     step(lambda x: start_ref[x], START, 1, pow_ref.at[0], V1)
     krylov(0)
-    flood(2)
     receive(V1)
     lower = step(lambda x: pow_ref[0, x], V1, 0, pow_ref.at[1], V2, zero)
     krylov(1)
@@ -333,9 +341,10 @@
     krylov, total = pl.pallas_call(
         functools.partial(kernel, sizes),
         out_shape=(jax.ShapeDtypeStruct((DEGREE, X, Y, S), f32), jax.ShapeDtypeStruct((8, S), f32)),
-        in_specs=[pl.BlockSpec(memory_space=pltpu.SMEM), vmem, vmem, vmem],
+        in_specs=[pl.BlockSpec(memory_space=pltpu.SMEM)] + [pl.BlockSpec(memory_space=pl.ANY)] * 3,
         out_specs=(pl.BlockSpec(memory_space=pl.ANY), vmem),
         scratch_shapes=[
+            *[pltpu.VMEM((X, Y, S), f32)] * 3,
             pltpu.VMEM((POWER - 1, X, Y, S), f32),
             pltpu.VMEM((DEGREE, X, Y, S), f32),
             pltpu.VMEM((X + 1, Y, S), f32),
@@ -349,6 +358,7 @@
             pltpu.SemaphoreType.DMA((len(stages),)),
             pltpu.SemaphoreType.DMA((DEGREE,)),
             pltpu.SemaphoreType.REGULAR((max(floods, 1),)),
+            pltpu.SemaphoreType.DMA((3,)),
         ],
         compiler_params=pltpu.CompilerParams(collective_id=0, has_side_effects=True),
     )(plane_counts, right_side, coefficient, start_vector)

time: 27.1 us -> 26.8 us (0.989)
  Pallas kernels: 26.3 us -> 26 us
    pallas_call x1, Pallas kernels: 24.3 us -> 24 us  [on_device(): pl.pallas_call(functools.partial(kernel, sizes), out_shape=(jax.ShapeDtyp...]
where the time goes in v3:
time: 26.8 us; the launch traced here: 26.7 us
  Pallas kernels  26 us (97%)
  between operations  0.64 us (2%)
    pallas_call x1, Pallas kernels, on_device(): pl.pallas_call(functools.partial(kernel, sizes), out_shape=(jax.ShapeDtyp...  24 us
    pallas_call x1, Pallas kernels, on_device(): pl.pallas_call(combine, out_shape=(jax.ShapeDtypeStruct((X, Y, S), f32),)...  2.05 us

profile of v3, /device:TPU:1, one launch (start us, length us, event | category | flops | bytes accessed | tf_op | source)
XLA Modules:
  0.0 26.7 jit_solution(8036306176942412978)
XLA Ops:
  0.6 24.0 %shard_map.59 = (f32[4,16,16,128]{3,2,1,0:T(8,128)}, f32[8,128]{1,0:T(8,128)}) custom-call(s32[4]{0:T(128)} %counts_ref.3, f32[16,16,128]{2,1,0:T(8,128)} %rhs_ref.1, f32[16,16,128]{2,1,0:T(8,128)} %coef_hbm.1, f32[16,16,128]{2,1,0:T(8,128)} %start_hbm.1), custom_call_target="tpu_custom_call" | custom-call | tf_op jit(solution)/shard_map/pallas_call | solution.py:341
  24.6 2.1 %shard_map.60 = (f32[16,16,128]{2,1,0:T(8,128)}, f32[16,16,128]{2,1,0:T(8,128)}) custom-call(s32[4]{0:T(128)} %counts_ref.3, f32[8,128]{1,0:T(8,128)} %get-tuple-element.4.total_ref, f32[16,16,128]{2,1,0:T(8,128)} %rhs_ref.1, f32[4,16,16,128]{3,2,1,0:T(8,128)} %get-tuple-element.5.kry_ref), custom_call_target="tpu_custom_call" | custom-call | tf_op jit(solution)/shard_map/pallas_call | solution.py:365

commit v4 on v3

--- a/solution.py
+++ b/solution.py
@@ -75,14 +75,13 @@
                         sem, inc=1, device_id={a: me[a] + (1 if side else -1)}, device_id_type=MESH
                     )
 
-    flooded = [0]
-
-    def flood(rounds):
-        for _ in range(rounds):
-            if flooded[0] < floods:
-                greet(flood_sem.at[flooded[0]])
-                pl.semaphore_wait(flood_sem.at[flooded[0]], neighbours)
-                flooded[0] += 1
+    def flood(i):
+        if i < floods:
+            greet(flood_sem.at[i])
+
+    def flood_wait(i):
+        if i < floods:
+            pl.semaphore_wait(flood_sem.at[i], neighbours)
 
     barrier = pltpu.get_barrier_semaphore()
     if floods:
@@ -242,6 +241,7 @@
         pack.put(1, x, start_ref[x])
     pack.finish()
     pl.semaphore_wait(barrier, arrivals)
+    flood(0)
     launch(START)
     loads[2].wait()
     pack = Packer(RIGHT)
@@ -261,15 +261,25 @@
         out_copy(i).start()
 
     zero = jnp.zeros((Y, S), jnp.float32)
-    flood(3)
+    flood_wait(0)
+    for i in range(1, floods - 2):
+        flood(i)
+        flood_wait(i)
     receive(START)
     weights(START)
     step(lambda x: start_ref[x], START, 1, pow_ref.at[0], V1)
     krylov(0)
     receive(V1)
+    if floods > 2:
+        flood(floods - 2)
     lower = step(lambda x: pow_ref[0, x], V1, 0, pow_ref.at[1], V2, zero)
+    if floods > 2:
+        flood_wait(floods - 2)
+    if floods > 1:
+        flood(floods - 1)
     krylov(1)
-    flood(floods)
+    if floods > 1:
+        flood_wait(floods - 1)
     receive(V2)
     upper = step(lambda x: pow_ref[1, x], V2, 0, None, None, zero)
 

time: 26.8 us -> 26.5 us (0.989); the launches traced: 26.7 us -> 26 us
  Pallas kernels: 26 us -> 25.4 us
    pallas_call x1, Pallas kernels: 24 us -> 23.3 us  [on_device(): pl.pallas_call(functools.partial(kernel, sizes), out_shape=(jax.ShapeDtyp...]
where the time goes in v4:
time: 26.5 us; the launch traced here: 26 us
  Pallas kernels  25.4 us (96%)
  between operations  0.64 us (2%)
    pallas_call x1, Pallas kernels, on_device(): pl.pallas_call(functools.partial(kernel, sizes), out_shape=(jax.ShapeDtyp...  23.3 us
    pallas_call x1, Pallas kernels, on_device(): pl.pallas_call(combine, out_shape=(jax.ShapeDtypeStruct((X, Y, S), f32),)...  2.05 us

profile of v4, /device:TPU:1, one launch (start us, length us, event | category | flops | bytes accessed | tf_op | source)
XLA Modules:
  0.0 26.0 jit_solution(6854886762992243289)
XLA Ops:
  0.6 23.3 %shard_map.59 = (f32[4,16,16,128]{3,2,1,0:T(8,128)}, f32[8,128]{1,0:T(8,128)}) custom-call(s32[4]{0:T(128)} %counts_ref.3, f32[16,16,128]{2,1,0:T(8,128)} %rhs_ref.1, f32[16,16,128]{2,1,0:T(8,128)} %coef_hbm.1, f32[16,16,128]{2,1,0:T(8,128)} %start_hbm.1), custom_call_target="tpu_custom_call" | custom-call | tf_op jit(solution)/shard_map/pallas_call | solution.py:351
  24.0 2.1 %shard_map.60 = (f32[16,16,128]{2,1,0:T(8,128)}, f32[16,16,128]{2,1,0:T(8,128)}) custom-call(s32[4]{0:T(128)} %counts_ref.3, f32[8,128]{1,0:T(8,128)} %get-tuple-element.4.total_ref, f32[16,16,128]{2,1,0:T(8,128)} %rhs_ref.1, f32[4,16,16,128]{3,2,1,0:T(8,128)} %get-tuple-element.5.kry_ref), custom_call_target="tpu_custom_call" | custom-call | tf_op jit(solution)/shard_map/pallas_call | solution.py:375
